TPU v7x, 128 devices: a whole 4x4x4 slice. The times are simulated.
128 devices in a mesh: rep: 1, data: 16 (over z, y), expert: 8 (over x, core).
Axes of the slice: x: 4, y: 4, z: 4, core: 2. Of those that a mesh axis runs over, the one named last changes fastest.
Arguments:
- x_tok: bfloat16 [49152, 2048], P(('rep', 'expert', 'data'))
- expert_idx: int32 [49152, 8], P(('rep', 'expert', 'data'))
- gate_val: float32 [49152, 8], P(('rep', 'expert', 'data'))
- w_gate: bfloat16 [128, 2048, 704], P('expert', 'data')
- w_up: bfloat16 [128, 2048, 704], P('expert', 'data')
- w_down: bfloat16 [128, 704, 2048], P('expert', None, 'data')
- ws_gate: bfloat16 [2048, 704], P(('expert', 'data'))
- ws_up: bfloat16 [2048, 704], P(('expert', 'data'))
- ws_down: bfloat16 [704, 2048], P(None, ('expert', 'data'))
Outputs:
- output: bfloat16 [49152, 2048], P(('rep', 'expert', 'data'))
All inputs are finite; a program needn't handle non-finite values.
Results may differ from a plain program's by a relative error of at most 0.00112.
Values are sent between devices in bfloat16 or wider.
A program may use at most 1 GiB of HBM per device.

v0:
```python
import jax
import jax.numpy as jnp
from jax import lax
from jax.sharding import PartitionSpec as P

CAP_NUM = 5
CAP_DEN = 4


def capacity_of(tok_count, top_count, n_exp):
    return max(8, ((CAP_NUM * top_count * tok_count) // (CAP_DEN * n_exp) + 7) // 8 * 8)


def local_dispatch(x_loc, idx_loc, n_local, exp_n, capacity):
    tok_count, top_count = idx_loc.shape
    pair_count = tok_count * top_count
    n_exp = n_local * exp_n
    flat_idx = idx_loc.reshape(pair_count)
    onehot = (flat_idx[:, None] == jnp.arange(n_exp, dtype=jnp.int32)[None, :]).astype(jnp.int32)
    slot_idx = jnp.sum((jnp.cumsum(onehot, axis=0) - onehot) * onehot, axis=1)
    kept_mask = slot_idx < capacity
    slot_pos = (flat_idx % n_local) * (exp_n * capacity) + (flat_idx // n_local) * capacity + slot_idx
    dest_pos = jnp.where(kept_mask, slot_pos, n_exp * capacity)
    src_pair = jnp.full((n_exp * capacity,), pair_count, jnp.int32).at[dest_pos].set(jnp.arange(pair_count, dtype=jnp.int32), mode="drop")
    tok_rows = jnp.take(x_loc, jnp.minimum(src_pair, pair_count - 1) // top_count, axis=0)
    buffer = jnp.where((src_pair < pair_count)[:, None], tok_rows, jnp.zeros((), x_loc.dtype))
    return buffer, dest_pos, kept_mask


def expert_swiglu(tok_rows, w_gate, w_up, w_down):
    gate_pre = jnp.einsum("ecd,edf->ecf", tok_rows, w_gate, preferred_element_type=jnp.float32)
    up_pre = jnp.einsum("ecd,edf->ecf", tok_rows, w_up, preferred_element_type=jnp.float32)
    hidden = (jax.nn.silu(gate_pre) * up_pre).astype(jnp.bfloat16)
    return jnp.einsum("ecf,efd->ecd", hidden, w_down, preferred_element_type=jnp.float32).astype(jnp.bfloat16)


def shared_swiglu(x_loc, ws_gate, ws_up, ws_down):
    gate_pre = jnp.dot(x_loc, ws_gate, preferred_element_type=jnp.float32)
    up_pre = jnp.dot(x_loc, ws_up, preferred_element_type=jnp.float32)
    hidden = (jax.nn.silu(gate_pre) * up_pre).astype(jnp.bfloat16)
    return jnp.dot(hidden, ws_down, preferred_element_type=jnp.float32)


def local_combine(x_loc, shared_f32, out_flat, dest_pos, kept_mask, gate_loc):
    tok_count, top_count = gate_loc.shape
    row_count = out_flat.shape[0]
    picked = jnp.take(out_flat, jnp.minimum(dest_pos, row_count - 1), axis=0)
    weight = jnp.where(kept_mask, gate_loc.reshape(tok_count * top_count), 0.0)
    routed = jnp.sum((weight[:, None] * picked).reshape(tok_count, top_count, -1), axis=1)
    return (x_loc.astype(jnp.float32) + shared_f32 + routed).astype(jnp.bfloat16)


def solution(mesh):
    exp_n = mesh.shape["expert"]
    tok_spec = P(("rep", "expert", "data"), None)
    group_axes = ("expert", "data")

    def device_fn(x_loc, idx_loc, gate_loc, wg_loc, wu_loc, wd_loc, wsg_loc, wsu_loc, wsd_loc):
        tok_count, d_model = x_loc.shape
        n_local = wg_loc.shape[0]
        capacity = capacity_of(tok_count, idx_loc.shape[1], n_local * exp_n)
        buffer, dest_pos, kept_mask = local_dispatch(x_loc, idx_loc, n_local, exp_n, capacity)
        received = lax.all_to_all(buffer.reshape(n_local, exp_n, capacity, d_model), "expert", 1, 1, tiled=True)
        w_gate = lax.all_gather(wg_loc, "data", axis=1, tiled=True)
        w_up = lax.all_gather(wu_loc, "data", axis=1, tiled=True)
        w_down = lax.all_gather(wd_loc, "data", axis=2, tiled=True)
        expert_out = expert_swiglu(received.reshape(n_local, exp_n * capacity, d_model), w_gate, w_up, w_down)
        returned = lax.all_to_all(expert_out.reshape(n_local, exp_n, capacity, d_model), "expert", 1, 1, tiled=True)
        ws_gate = lax.all_gather(wsg_loc, group_axes, axis=0, tiled=True)
        ws_up = lax.all_gather(wsu_loc, group_axes, axis=0, tiled=True)
        ws_down = lax.all_gather(wsd_loc, group_axes, axis=1, tiled=True)
        shared_f32 = shared_swiglu(x_loc, ws_gate, ws_up, ws_down)
        return local_combine(x_loc, shared_f32, returned.reshape(n_local * exp_n * capacity, d_model), dest_pos, kept_mask, gate_loc)

    in_specs = (tok_spec, tok_spec, tok_spec, P("expert", "data", None), P("expert", "data", None), P("expert", None, "data"), P(group_axes, None), P(group_axes, None), P(None, group_axes))
    return jax.shard_map(device_fn, mesh=mesh, in_specs=in_specs, out_specs=tok_spec, check_vma=False)
```

profile of v0, /device:TPU:1, one launch (start us, length us, event | category | flops | bytes accessed | tf_op | source)
XLA Modules:
  0.0 1158.1 jit_solution(4629071423636411328)
XLA Ops:
  6.5 0.7 all-gather.13.cloned.1.call-update
  7.3 0.7 all-gather.15.cloned.1.call-update
  8.1 0.7 all-gather.17.cloned.1.call-update
  10.6 1.9 fusion.5
  12.5 0.7 compare_select_fusion.1
  13.3 11.8 %scatter_custom_fusion = s32[4096]{0:T(1024)S(1)} fusion(s32[3072]{0:T(1024)S(1)} %bitcast.43, s32[3072]{0:T(1024)S(1)} %iota.11, s32[]{:T(128)} %constant.90.clone.1), kind=kCustom, calls=%fused_computation.67 | custom fusion | bytes 16388 | tf_op jit(solution)/shard_map/scatter | solution.py:24
  25.4 20.9 %gather_fusion = bf16[4096,2048]{1,0:T(8,128)(2,1)} fusion(bf16[384,2048]{1,0:T(8,128)(2,1)S(1)} %copy-done, s32[4096]{0:T(1024)S(1)} %broadcast_clamp_fusion), kind=kCustom, calls=%fused_computation | custom fusion | bytes 33570816 | tf_op jit(solution)/shard_map/jit(_take)/gather | solution.py:25
  46.3 14.4 %fusion = bf16[16,8,32,2048]{3,2,0,1:T(8,128)(2,1)} fusion(bf16[16,8,32,2048]{3,2,1,0:T(8,128)(2,1)} %bitcast.37, pred[16,8,32]{2,0,1:T(8,128)(4,1)S(1)} %copy.47, pred[16,8,32]{2,0,1:T(8,128)(4,1)S(1)} %copy.46), kind=kLoop, calls=%fused_computation.5 | loop fusion | flops 16777216 | bytes 33562624 | tf_op jit(solution)/shard_map/jit(_where)/select_n | solution.py:26
  60.7 7.0 all-to-all-start
  68.2 182.9 %all-to-all-done = bf16[16,8,32,2048]{3,2,0,1:T(8,128)(2,1)} async-done(((bf16[16,8,32,2048]{3,2,0,1:T(8,128)(2,1)}), bf16[16,8,32,2048]{3,2,0,1:T(8,128)(2,1)}, u32[]{:S(2)}, u32[]{:S(2)}) %all-to-all-start) | async-done | bytes 16777248 | tf_op jit(solution)/shard_map/all_to_all | solution.py:63
  251.1 14.1 %copy.49 = bf16[16,8,32,2048]{3,2,1,0:T(8,128)(2,1)} copy(bf16[16,8,32,2048]{3,2,0,1:T(8,128)(2,1)} %all-to-all-done) | data formatting | bytes 33554432 | tf_op jit(solution)/shard_map/all_to_all | solution.py:63
  265.2 14.8 %all-gather.13.cloned.1.call-done = bf16[16,2048,704]{1,2,0:T(8,128)(2,1)} async-done(((bf16[16,128,704]{1,2,0:T(8,128)(2,1)}), bf16[16,2048,704]{1,2,0:T(8,128)(2,1)}) %all-gather.13.cloned.1.call-update) | async-done | bytes 46137360 | tf_op jit(solution)/shard_map/all_gather | solution.py:64
  280.0 27.0 %fusion.31 = f32[16,256,704]{1,2,0:T(8,128)} fusion(bf16[16,256,2048]{2,1,0:T(8,128)(2,1)} %bitcast.38, bf16[16,2048,704]{1,2,0:T(8,128)(2,1)} %all-gather.13.cloned.1.call-done), kind=kOutput, calls=%fused_computation.73 | convolution fusion | flops 11811160064 | bytes 74448896 | tf_op jit(solution)/shard_map/ecd,edf->ecf/dot_general | solution.py:31
  307.0 243.1 %all-gather.15.cloned.1.call-done = bf16[16,2048,704]{1,2,0:T(8,128)(2,1)} async-done(((bf16[16,128,704]{1,2,0:T(8,128)(2,1)}), bf16[16,2048,704]{1,2,0:T(8,128)(2,1)}) %all-gather.15.cloned.1.call-update) | async-done | bytes 46137360 | tf_op jit(solution)/shard_map/all_gather | solution.py:65
  550.2 270.1 %all-gather.17.cloned.1.call-done = bf16[16,704,2048]{2,1,0:T(8,128)(2,1)} async-done(((bf16[16,704,128]{2,1,0:T(8,128)(2,1)}), bf16[16,704,2048]{2,1,0:T(8,128)(2,1)}) %all-gather.17.cloned.1.call-update) | async-done | bytes 46137360 | tf_op jit(solution)/shard_map/all_gather | solution.py:66
  820.3 45.8 %convolution_convert_fusion = bf16[16,256,2048]{2,1,0:T(8,128)(2,1)} fusion(bf16[16,704,2048]{2,1,0:T(8,128)(2,1)} %all-gather.17.cloned.1.call-done, f32[16,256,704]{1,2,0:T(8,128)} %fusion.31, bf16[16,256,2048]{2,1,0:T(8,128)(2,1)} %bitcast.39, bf16[16,2048,704]{1,2,0:T(8,128)(2,1)} %all-gather.15.cloned.1.call-done), kind=kOutput, calls=%fused_computation.6 | convolution fusion | flops 23648010240 | bytes 137363456 | tf_op jit(solution)/shard_map/ecf,efd->ecd/dot_general | solution.py:34
  866.1 14.1 %copy.50 = bf16[16,8,32,2048]{3,2,0,1:T(8,128)(2,1)} copy(bf16[16,8,32,2048]{3,2,1,0:T(8,128)(2,1)} %bitcast.40) | data formatting | bytes 33554432 | tf_op jit(solution)/shard_map/reshape | solution.py:68
  880.2 7.8 all-to-all-start.1
  890.1 3.6 fusion.30
  893.7 188.9 %all-to-all-done.1 = bf16[16,8,32,2048]{3,2,0,1:T(8,128)(2,1)} async-done(((bf16[16,8,32,2048]{3,2,0,1:T(8,128)(2,1)}), bf16[16,8,32,2048]{3,2,0,1:T(8,128)(2,1)}, u32[]{:S(2)}, u32[]{:S(2)}) %all-to-all-start.1) | async-done | bytes 16777248 | tf_op jit(solution)/shard_map/all_to_all | solution.py:68
  1082.6 14.1 %copy.51 = bf16[16,8,32,2048]{3,2,1,0:T(8,128)(2,1)} copy(bf16[16,8,32,2048]{3,2,0,1:T(8,128)(2,1)} %all-to-all-done.1) | data formatting | bytes 33554432 | tf_op jit(solution)/shard_map/all_to_all | solution.py:68
  1096.7 31.8 %gather_fusion.1 = bf16[3072,2048]{1,0:T(8,128)(2,1)} fusion(bf16[4096,2048]{1,0:T(8,128)(2,1)} %bitcast.36, s32[3072]{0:T(1024)S(1)} %broadcast_clamp_fusion.1), kind=kCustom, calls=%fused_computation.1 | custom fusion | bytes 25178112 | tf_op jit(solution)/shard_map/jit(_take)/gather | solution.py:47
  1128.5 14.8 %multiply_reduce_fusion = f32[384,2048]{1,0:T(8,128)} fusion(bf16[3072,2048]{1,0:T(8,128)(2,1)} %gather_fusion.1, f32[384,8]{1,0:T(8,128)S(1)} %broadcast_select_fusion, pred[384,8]{1,0:T(8,128)(4,1)S(1)} %compare_and_fusion), kind=kLoop, calls=%fused_computation.3 | loop fusion | flops 24379392 | bytes 15744000 | tf_op jit(solution)/shard_map/reduce_sum | solution.py:49
  1143.3 8.0 add_convert_fusion
  (52 shorter events, 4.8 us)
Async XLA Ops:
  6.5 2.2 copy-start.6
  6.5 273.5 %all-gather.13.cloned.1.call-start = ((), (), s32[]{:S(2)}) async-start(), calls=%async_computation.5 | async-start | bytes 49020928 | tf_op jit(solution)/shard_map/all_gather | solution.py:64
  7.3 542.9 %all-gather.15.cloned.1.call-start = ((), (), s32[]{:S(2)}) async-start(), calls=%async_computation.6 | async-start | bytes 49020928 | tf_op jit(solution)/shard_map/all_gather | solution.py:65
  8.0 812.3 %all-gather.17.cloned.1.call-start = ((), (), s32[]{:S(2)}) async-start(), calls=%async_computation.7 | async-start | bytes 49020928 | tf_op jit(solution)/shard_map/all_gather | solution.py:66
  8.8 16.6 %copy-start = (bf16[384,2048]{1,0:T(8,128)(2,1)S(1)}, bf16[384,2048]{1,0:T(8,128)(2,1)}, u32[]{:S(2)}) copy-start(bf16[384,2048]{1,0:T(8,128)(2,1)} %param.9) | copy-start | bytes 4718596
  8.9 0.7 copy-start.1
  12.5 0.8 copy-start.3
  60.7 190.4 %all-to-all-start = ((bf16[16,8,32,2048]{3,2,0,1:T(8,128)(2,1)}), bf16[16,8,32,2048]{3,2,0,1:T(8,128)(2,1)}, u32[]{:S(2)}, u32[]{:S(2)}) async-start(bf16[16,8,32,2048]{3,2,0,1:T(8,128)(2,1)} %fusion), calls=%async_computation | async-start | bytes 33554432 | tf_op jit(solution)/shard_map/all_to_all | solution.py:63
  67.7 822.4 %all-gather.7.cloned.1.call-start = ((), (), s32[]{:S(2)}) async-start(), calls=%async_computation.2 | async-start | bytes 3170304 | tf_op jit(solution)/shard_map/all_gather | solution.py:69
  880.2 9.0 copy-start.4
  880.2 9.1 copy-start.7
  880.2 9.3 copy-start.5
  880.2 9.3 copy-start.2
  880.2 202.5 %all-to-all-start.1 = ((bf16[16,8,32,2048]{3,2,0,1:T(8,128)(2,1)}), bf16[16,8,32,2048]{3,2,0,1:T(8,128)(2,1)}, u32[]{:S(2)}, u32[]{:S(2)}) async-start(bf16[16,8,32,2048]{3,2,0,1:T(8,128)(2,1)} %copy.50), calls=%async_computation.1 | async-start | bytes 33554432 | tf_op jit(solution)/shard_map/all_to_all | solution.py:68
  888.0 255.3 %all-gather.11.cloned.1.call-start = ((), (), s32[]{:S(2)}) async-start(), calls=%async_computation.4 | async-start | bytes 3170304 | tf_op jit(solution)/shard_map/all_gather | solution.py:71
  888.6 254.7 %all-gather.9.cloned.1.call-start = ((), (), s32[]{:S(2)}) async-start(), calls=%async_computation.3 | async-start | bytes 3170304 | tf_op jit(solution)/shard_map/all_gather | solution.py:70
Sparse Core Ops, SparseCore 0:
  9.4 270.5 all-gather.12
  282.1 267.9 all-gather.14
  552.3 267.9 all-gather.16
  823.2 66.8 all-gather.6
  893.1 66.5 all-gather.10
  962.6 67.6 all-gather.8
where the time goes:
time: 1160 us
  waiting for transfers between devices  904 us (78%)
  local copies, waits for them, and re-layouts  108 us (9%)
  matrix products  84.3 us (7%)
  other arithmetic  32.7 us (3%)
  starting transfers between devices  15.1 us (1%)
  between operations  13.7 us (1%)
    all_gather x1, waiting for transfers between devices, device_fn(): w_down = lax.all_gather(wd_loc, 'data', axis=2, tiled=True)  270 us
    all_gather x1, waiting for transfers between devices, device_fn(): w_up = lax.all_gather(wu_loc, 'data', axis=1, tiled=True)  243 us
    all_to_all x1, waiting for transfers between devices, device_fn(): lax.all_to_all(expert_out.reshape(n_local, exp_n, capacity, d_model), 'ex...  189 us
    all_to_all x1, waiting for transfers between devices, device_fn(): lax.all_to_all(buffer.reshape(n_local, exp_n, capacity, d_model), 'expert...  183 us
    dot_general x1, matrix products, expert_swiglu(): jnp.einsum('ecf,efd->ecd', hidden, w_down, preferred_element_type=jnp.flo...  45.8 us
    gather x1, local copies, waits for them, and re-layouts, local_combine(): picked = jnp.take(out_flat, jnp.minimum(dest_pos, row_count - 1), axis=0)  31.8 us
    dot_general x1, matrix products, expert_swiglu(): jnp.einsum('ecd,edf->ecf', tok_rows, w_gate, preferred_element_type=jnp.f...  27 us
  transfers between devices with their start and end apart: 8, of which 6 were waited for; matrix products, arithmetic and copies ran while one was open for 19% of the time, Pallas kernels for 0%

commit v1 on v0

v1 whole, which is shorter than its diff:
```python
import jax
import jax.numpy as jnp
from jax import lax
from jax.sharding import PartitionSpec as P

CAP_NUM = 5
CAP_DEN = 4


def capacity_of(tok_count, top_count, n_exp):
    return max(8, ((CAP_NUM * top_count * tok_count) // (CAP_DEN * n_exp) + 7) // 8 * 8)


def routing(idx_loc, gate_loc, n_exp, capacity):
    tok_count = idx_loc.shape[0]
    hit = idx_loc[:, :, None] == jnp.arange(n_exp, dtype=jnp.int32)[None, None, :]
    chosen = jnp.any(hit, axis=1)
    gates = jnp.sum(jnp.where(hit, gate_loc[:, :, None], 0.0), axis=1)
    before = jnp.tril(jnp.ones((tok_count, tok_count), jnp.bfloat16), -1)
    slot = jnp.dot(before, chosen.astype(jnp.bfloat16), preferred_element_type=jnp.float32).astype(jnp.int32)
    slot = jnp.where(chosen & (slot < capacity), slot, capacity)
    return slot.T, gates.T


def split3(val):
    hi = lax.reduce_precision(val, 8, 7)
    mid = lax.reduce_precision(val - hi, 8, 7)
    low = val - hi - mid
    return [part.astype(jnp.bfloat16) for part in (hi, mid, low)]


def solution(mesh):
    exp_n = mesh.shape["expert"]
    data_n = mesh.shape["data"]
    tok_spec = P(("rep", "expert", "data"), None)
    group_axes = ("expert", "data")

    def device_fn(x_loc, idx_loc, gate_loc, wg_loc, wu_loc, wd_loc, wsg_loc, wsu_loc, wsd_loc):
        tok_count, d_model = x_loc.shape
        n_exp = wg_loc.shape[0] * exp_n
        ff = wg_loc.shape[2]
        capacity = capacity_of(tok_count, idx_loc.shape[1], n_exp)
        w_gate = lax.all_to_all(wg_loc, "data", 0, 1, tiled=True).reshape(d_model, ff)
        w_up = lax.all_to_all(wu_loc, "data", 0, 1, tiled=True).reshape(d_model, ff)
        w_down = lax.all_to_all(wd_loc, "data", 0, 0, tiled=True)
        w_down = w_down.reshape(data_n, ff, d_model // data_n)
        slot, gates = routing(idx_loc, gate_loc, n_exp, capacity)
        sel = slot[:, None, :] == jnp.arange(capacity, dtype=jnp.int32)[None, :, None]
        pick = sel.astype(jnp.bfloat16).reshape(n_exp * capacity, tok_count)
        buffer = jnp.dot(pick, x_loc, preferred_element_type=jnp.float32).astype(jnp.bfloat16)
        received = lax.all_to_all(buffer.reshape(n_exp, capacity, d_model), group_axes, 0, 0, tiled=True)
        rows = received.reshape(n_exp * capacity, d_model)
        gate_pre = jnp.dot(rows, w_gate, preferred_element_type=jnp.float32)
        up_pre = jnp.dot(rows, w_up, preferred_element_type=jnp.float32)
        hidden = (jax.nn.silu(gate_pre) * up_pre).astype(jnp.bfloat16)
        w_down = jnp.transpose(w_down, (1, 0, 2)).reshape(ff, d_model)
        expert_out = jnp.dot(hidden, w_down, preferred_element_type=jnp.float32).astype(jnp.bfloat16)
        returned = lax.all_to_all(expert_out.reshape(n_exp, capacity, d_model), group_axes, 0, 0, tiled=True)
        returned = returned.reshape(n_exp * capacity, d_model)
        ws_gate = lax.all_gather(wsg_loc, group_axes, axis=0, tiled=True)
        ws_up = lax.all_gather(wsu_loc, group_axes, axis=0, tiled=True)
        ws_down = lax.all_gather(wsd_loc, group_axes, axis=1, tiled=True)
        s_gate = jnp.dot(x_loc, ws_gate, preferred_element_type=jnp.float32)
        s_up = jnp.dot(x_loc, ws_up, preferred_element_type=jnp.float32)
        s_hidden = (jax.nn.silu(s_gate) * s_up).astype(jnp.bfloat16)
        total = jnp.dot(s_hidden, ws_down, preferred_element_type=jnp.float32) + x_loc.astype(jnp.float32)
        for part in split3(gates):
            weight = jnp.where(sel, part[:, None, :], jnp.zeros((), jnp.bfloat16)).reshape(n_exp * capacity, tok_count)
            total += lax.dot_general(weight, returned, (((0,), (0,)), ((), ())), preferred_element_type=jnp.float32)
        return total.astype(jnp.bfloat16)

    in_specs = (tok_spec, tok_spec, tok_spec, P("expert", "data", None), P("expert", "data", None), P("expert", None, "data"), P(group_axes, None), P(group_axes, None), P(None, group_axes))
    return jax.shard_map(device_fn, mesh=mesh, in_specs=in_specs, out_specs=tok_spec, check_vma=False)
```

time: 1160 us -> 715 us (0.62)
  waiting for transfers between devices: 904 us -> 505 us
  local copies, waits for them, and re-layouts: 108 us -> 0.86 us
  blocking collectives: 0 us -> 45.6 us
  other arithmetic: 32.7 us -> 4.99 us
  matrix products: 84.3 us -> 110 us
  starting transfers between devices: 15.1 us -> 35.1 us
    all_gather x3 -> x0, waiting for transfers between devices: 528 us -> none  [the longest x1 270 us: device_fn(): w_down = lax.all_gather(wd_loc, 'data', axis=2, tiled=True)]
    all_gather x1, waiting for transfers between devices: 0.01 us -> 128 us  [device_fn(): ws_up = lax.all_gather(wsu_loc, group_axes, axis=0, tiled=True)]
    all_gather x1, waiting for transfers between devices: 0.01 us -> 103 us  [device_fn(): ws_down = lax.all_gather(wsd_loc, group_axes, axis=1, tiled=True)]
    all_to_all x2 -> x4, waiting for transfers between devices: 372 us -> 271 us  [the longest x1 232 us: device_fn(): lax.all_to_all(buffer.reshape(n_exp, capacity, d_model), group_axes, 0, 0...]
    gather x2 -> x0, local copies, waits for them, and re-layouts: 52.7 us -> none  [the longest x1 31.8 us: local_combine(): picked = jnp.take(out_flat, jnp.minimum(dest_pos, row_count - 1), axis=0)]
    all_to_all x0 -> x1, blocking collectives: none -> 45.6 us  [device_fn(): lax.all_to_all(wg_loc, 'data', 0, 1, tiled=True).reshape(d_model, ff)]
    all_to_all x2 -> x0, local copies, waits for them, and re-layouts: 28.2 us -> none  [the longest x1 14.1 us: device_fn(): lax.all_to_all(buffer.reshape(n_local, exp_n, capacity, d_model), 'expert...]
    dot_general x4 -> x9, matrix products: 84.3 us -> 110 us  [the longest x3 32.3 us: device_fn(): lax.dot_general(weight, returned, (((0,), (0,)), ((), ())), preferred_ele...]
  transfers between devices with their start and end apart: 8 -> 7, of which waited for: 6 -> 5; matrix products, arithmetic and copies ran while one was open for 19% -> 12% of each run, Pallas kernels for 0% -> 0%
where the time goes in v1:
time: 715 us
  waiting for transfers between devices  505 us (71%)
  matrix products  110 us (15%)
  blocking collectives  45.6 us (6%)
  starting transfers between devices  35.1 us (5%)
  between operations  13.3 us (2%)
    all_to_all x1, waiting for transfers between devices, device_fn(): lax.all_to_all(buffer.reshape(n_exp, capacity, d_model), group_axes, 0, 0...  232 us
    all_gather x1, waiting for transfers between devices, device_fn(): ws_up = lax.all_gather(wsu_loc, group_axes, axis=0, tiled=True)  128 us
    all_gather x1, waiting for transfers between devices, device_fn(): ws_down = lax.all_gather(wsd_loc, group_axes, axis=1, tiled=True)  103 us
    all_to_all x1, blocking collectives, device_fn(): lax.all_to_all(wg_loc, 'data', 0, 1, tiled=True).reshape(d_model, ff)  45.6 us
    dot_general x3, matrix products, device_fn(): lax.dot_general(weight, returned, (((0,), (0,)), ((), ())), preferred_ele...  32.3 us
    dot_general x1, matrix products, device_fn(): jnp.dot(hidden, w_down, preferred_element_type=jnp.float32)  32.2 us
    all_to_all x1, waiting for transfers between devices, device_fn(): w_up = lax.all_to_all(wu_loc, 'data', 0, 1, tiled=True).reshape(d_model, ff)  24.2 us
    dot_general x1, matrix products, device_fn(): gate_pre = jnp.dot(rows, w_gate, preferred_element_type=jnp.float32)  19.3 us
  transfers between devices with their start and end apart: 7, of which 5 were waited for; matrix products, arithmetic and copies ran while one was open for 12% of the time, Pallas kernels for 0%

profile of v1, /device:TPU:1, one launch (start us, length us, event | category | flops | bytes accessed | tf_op | source)
XLA Modules:
  0.0 714.8 jit_solution(6499899901928026275)
XLA Ops:
  6.5 45.6 %all_to_all.33 = bf16[16,128,704]{1,2,0:T(8,128)(2,1)} all-to-all(bf16[16,128,704]{1,2,0:T(8,128)(2,1)} %param.12), channel_id=1, replica_groups=mesh['rep'=1,'data'=16,'expert'=8] {'data'}, dimensions={0} | all-to-all | bytes 5767168 | tf_op jit(solution)/shard_map/all_to_all | solution.py:43
  52.2 4.1 all-to-all-start.2
  56.4 2.0 fusion.31
  59.0 1.0 bitcast_compare_fusion
  60.1 13.8 %convolution_convert_fusion.1 = bf16[4096,2048]{1,0:T(8,128)(2,1)} fusion(pred[4096,384]{1,0:T(32,128)(4,1)S(1)} %bitcast_compare_fusion, bf16[384,2048]{1,0:T(8,128)(2,1)} %param.9), kind=kOutput, calls=%fused_computation.1 | convolution fusion | flops 6450839552 | bytes 19922944 | tf_op jit(solution)/shard_map/dot_general | solution.py:50
  73.9 24.2 %all-to-all-done.2 = bf16[16,128,704]{1,2,0:T(8,128)(2,1)S(1)} async-done(((bf16[16,128,704]{1,2,0:T(8,128)(2,1)}), bf16[16,128,704]{1,2,0:T(8,128)(2,1)S(1)}, u32[]{:S(2)}, u32[]{:S(2)}) %all-to-all-start.2) | async-done | bytes 2883616 | tf_op jit(solution)/shard_map/all_to_all | solution.py:44
  98.0 8.1 %all-to-all-start = ((bf16[128,32,2048]{2,1,0:T(8,128)(2,1)}), bf16[128,32,2048]{2,1,0:T(8,128)(2,1)}, u32[]{:S(2)}, u32[]{:S(2)}) async-start(bf16[128,32,2048]{2,1,0:T(8,128)(2,1)} %bitcast.65), calls=%async_computation | async-start | bytes 33554432 | tf_op jit(solution)/shard_map/all_to_all | solution.py:51
  106.2 0.7 all-gather.4.cloned.1.call-update
  106.9 231.7 %all-to-all-done = bf16[128,32,2048]{2,1,0:T(8,128)(2,1)} async-done(((bf16[128,32,2048]{2,1,0:T(8,128)(2,1)}), bf16[128,32,2048]{2,1,0:T(8,128)(2,1)}, u32[]{:S(2)}, u32[]{:S(2)}) %all-to-all-start) | async-done | bytes 16777248 | tf_op jit(solution)/shard_map/all_to_all | solution.py:51
  338.6 6.6 all-to-all-start.3
  345.2 19.3 %fusion.22 = f32[4096,704]{0,1:T(8,128)} fusion(bf16[4096,2048]{1,0:T(8,128)(2,1)} %bitcast.4, bf16[16,128,704]{1,2,0:T(8,128)(2,1)} %all_to_all.33), kind=kOutput, calls=%fused_computation.23 | convolution fusion | flops 11811160064 | bytes 31195136 | tf_op jit(solution)/shard_map/dot_general | solution.py:53
  364.5 15.5 %all-to-all-done.3 = bf16[16,704,128]{2,1,0:T(8,128)(2,1)} async-done(((bf16[16,704,128]{2,1,0:T(8,128)(2,1)}), bf16[16,704,128]{2,1,0:T(8,128)(2,1)}, u32[]{:S(2)}, u32[]{:S(2)}) %all-to-all-start.3) | async-done | bytes 2883616 | tf_op jit(solution)/shard_map/all_to_all | solution.py:45
  380.0 32.2 %convolution_convert_fusion = bf16[4096,2048]{1,0:T(8,128)(2,1)} fusion(f32[4096,704]{0,1:T(8,128)} %fusion.22, bf16[4096,2048]{1,0:T(8,128)(2,1)} %bitcast.4, bf16[16,704,128]{2,1,0:T(8,128)(2,1)} %all-to-all-done.3, bf16[16,128,704]{1,2,0:T(8,128)(2,1)S(1)} %all-to-all-done.2), kind=kOutput, calls=%fused_computation | convolution fusion | flops 23648010240 | bytes 50855936 | tf_op jit(solution)/shard_map/dot_general | solution.py:57
  412.2 15.9 %all-to-all-start.4 = ((bf16[128,32,2048]{2,1,0:T(8,128)(2,1)}), bf16[128,32,2048]{2,1,0:T(8,128)(2,1)}, u32[]{:S(2)}, u32[]{:S(2)}) async-start(bf16[128,32,2048]{2,1,0:T(8,128)(2,1)} %bitcast.64), calls=%async_computation.4 | async-start | bytes 33554432 | tf_op jit(solution)/shard_map/all_to_all | solution.py:58
  428.1 0.7 all-gather.6.cloned.1.call-update
  429.1 0.5 all-gather.8.cloned.1.call-update
  429.7 1.9 select_reduce_fusion
  432.1 4.6 fusion.52
  436.7 128.0 %all-gather.6.cloned.1.call-done = bf16[2048,704]{1,0:T(8,128)(2,1)} async-done(((bf16[16,704]{1,0:T(8,128)(2,1)}), bf16[2048,704]{1,0:T(8,128)(2,1)}) %all-gather.6.cloned.1.call-update) | async-done | bytes 2883600 | tf_op jit(solution)/shard_map/all_gather | solution.py:61
  564.6 103.4 %all-gather.8.cloned.1.call-done = bf16[704,2048]{0,1:T(8,128)(2,1)} async-done(((bf16[704,16]{0,1:T(8,128)(2,1)}), bf16[704,2048]{0,1:T(8,128)(2,1)}) %all-gather.8.cloned.1.call-update) | async-done | bytes 2883600 | tf_op jit(solution)/shard_map/all_gather | solution.py:62
  668.0 7.9 %fusion.33 = f32[384,2048]{1,0:T(8,128)} fusion(bf16[704,2048]{0,1:T(8,128)(2,1)} %all-gather.8.cloned.1.call-done, bf16[384,2048]{1,0:T(8,128)(2,1)S(1)} %copy-done.2, bf16[2048,704]{1,0:T(8,128)(2,1)} %all-gather.6.cloned.1.call-done, f32[384,704]{0,1:T(8,128)} %fusion.52), kind=kOutput, calls=%fused_computation.38 | convolution fusion | flops 2216214528 | bytes 11567104 | tf_op jit(solution)/shard_map/dot_general | solution.py:66
  675.9 10.3 %fusion.4 = f32[384,2048,1]{1,0,2:T(8,128)S(1)} fusion(bf16[128,32,2048]{2,1,0:T(8,128)(2,1)} %all-to-all-done.4, s32[128,384]{1,0:T(8,128)S(1)} %fusion.39, bf16[128,384]{1,0:T(8,128)(2,1)S(1)} %copy.31), kind=kOutput, calls=%fused_computation.9 | convolution fusion | flops 6445596672 | bytes 20217856 | tf_op jit(solution)/shard_map/dot_general | solution.py:69
  686.2 10.4 %fusion.6 = f32[384,2048,1]{1,0,2:T(8,128)S(1)} fusion(bf16[128,32,2048]{2,1,0:T(8,128)(2,1)} %all-to-all-done.4, s32[128,384]{1,0:T(8,128)S(1)} %fusion.39, bf16[128,384]{1,0:T(8,128)(2,1)S(1)} %copy.35), kind=kOutput, calls=%fused_computation.10 | convolution fusion | flops 6445596672 | bytes 20217856 | tf_op jit(solution)/shard_map/dot_general | solution.py:69
  696.6 11.6 %fusion.10 = bf16[384,2048]{1,0:T(8,128)(2,1)} fusion(f32[384,2048,1]{1,0,2:T(8,128)S(1)} %fusion.6, f32[384,2048,1]{1,0,2:T(8,128)S(1)} %fusion.4, f32[384,2048]{1,0:T(8,128)S(1)} %copy-done.3, bf16[384,2048]{1,0:T(8,128)(2,1)S(1)} %copy-done.2, bf16[128,32,2048]{2,1,0:T(8,128)(2,1)} %all-to-all-done.4, s32[128,384]{1,0:T(8,128)S(1)} %fusion.39, ...), kind=kOutput, calls=%fused_computation.13 | convolution fusion | flops 6450315264 | bytes 29655040 | tf_op jit(solution)/shard_map/dot_general | solution.py:69
  (24 shorter events, 1.6 us)
Async XLA Ops:
  52.2 4.1 copy-start
  52.2 45.8 %all-to-all-start.2 = ((bf16[16,128,704]{1,2,0:T(8,128)(2,1)}), bf16[16,128,704]{1,2,0:T(8,128)(2,1)S(1)}, u32[]{:S(2)}, u32[]{:S(2)}) async-start(bf16[16,128,704]{1,2,0:T(8,128)(2,1)} %param.13), calls=%async_computation.2 | async-start | bytes 5767168 | tf_op jit(solution)/shard_map/all_to_all | solution.py:44
  98.0 240.5 %all-to-all-start = ((bf16[128,32,2048]{2,1,0:T(8,128)(2,1)}), bf16[128,32,2048]{2,1,0:T(8,128)(2,1)}, u32[]{:S(2)}, u32[]{:S(2)}) async-start(bf16[128,32,2048]{2,1,0:T(8,128)(2,1)} %bitcast.65), calls=%async_computation | async-start | bytes 33554432 | tf_op jit(solution)/shard_map/all_to_all | solution.py:51
  106.2 325.9 %all-gather.4.cloned.1.call-start = ((), (), s32[]{:S(2)}) async-start(), calls=%async_computation.5 | async-start | bytes 3170304 | tf_op jit(solution)/shard_map/all_gather | solution.py:60
  338.6 41.4 %all-to-all-start.3 = ((bf16[16,704,128]{2,1,0:T(8,128)(2,1)}), bf16[16,704,128]{2,1,0:T(8,128)(2,1)}, u32[]{:S(2)}, u32[]{:S(2)}) async-start(bf16[16,704,128]{2,1,0:T(8,128)(2,1)} %param.14), calls=%async_computation.3 | async-start | bytes 5767168 | tf_op jit(solution)/shard_map/all_to_all | solution.py:45
  412.2 17.4 %copy-start.1 = (f32[384,8]{0,1:T(8,128)S(1)}, f32[384,8]{0,1:T(8,128)}, u32[]{:S(2)}) copy-start(f32[384,8]{0,1:T(8,128)} %param.11) | copy-start | bytes 36868
  412.2 19.9 %copy-start.2 = (bf16[384,2048]{1,0:T(8,128)(2,1)S(1)}, bf16[384,2048]{1,0:T(8,128)(2,1)}, u32[]{:S(2)}) copy-start(bf16[384,2048]{1,0:T(8,128)(2,1)} %param.9) | copy-start | bytes 4718596
  412.2 263.7 %all-to-all-start.4 = ((bf16[128,32,2048]{2,1,0:T(8,128)(2,1)}), bf16[128,32,2048]{2,1,0:T(8,128)(2,1)}, u32[]{:S(2)}, u32[]{:S(2)}) async-start(bf16[128,32,2048]{2,1,0:T(8,128)(2,1)} %bitcast.64), calls=%async_computation.4 | async-start | bytes 33554432 | tf_op jit(solution)/shard_map/all_to_all | solution.py:58
  428.1 136.5 %all-gather.6.cloned.1.call-start = ((), (), s32[]{:S(2)}) async-start(), calls=%async_computation.6 | async-start | bytes 3170304 | tf_op jit(solution)/shard_map/all_gather | solution.py:61
  428.8 239.2 %all-gather.8.cloned.1.call-start = ((), (), s32[]{:S(2)}) async-start(), calls=%async_computation.7 | async-start | bytes 3170304 | tf_op jit(solution)/shard_map/all_gather | solution.py:62
  686.2 10.5 %copy-start.3 = (f32[384,2048]{1,0:T(8,128)S(1)}, f32[384,2048]{1,0:T(8,128)}, u32[]{:S(2)}) copy-start(f32[384,2048]{1,0:T(8,128)} %fusion.33) | copy-start | bytes 9437188
Sparse Core Ops, SparseCore 0:
  110.1 135.3 all-gather.3
  432.0 132.5 all-gather.5
  567.7 100.2 all-gather.7

commit v2 on v1

v2 whole, which is shorter than its diff:
```python
import jax
import jax.numpy as jnp
from jax import lax
from jax.experimental import pallas as pl
from jax.experimental.pallas import tpu as pltpu
from jax.sharding import PartitionSpec as P

MESH = pl.DeviceIdType.MESH
CAP_NUM = 5
CAP_DEN = 4
SIDE = 4


def capacity_of(tok_count, top_count, n_exp):
    return max(8, ((CAP_NUM * top_count * tok_count) // (CAP_DEN * n_exp) + 7) // 8 * 8)


def routing(idx_loc, gate_loc, n_exp, capacity):
    tok_count = idx_loc.shape[0]
    hit = idx_loc[:, :, None] == jnp.arange(n_exp, dtype=jnp.int32)[None, None, :]
    chosen = jnp.any(hit, axis=1)
    gates = jnp.sum(jnp.where(hit, gate_loc[:, :, None], 0.0), axis=1)
    before = jnp.tril(jnp.ones((tok_count, tok_count), jnp.bfloat16), -1)
    slot = jnp.dot(before, chosen.astype(jnp.bfloat16), preferred_element_type=jnp.float32).astype(jnp.int32)
    slot = jnp.where(chosen & (slot < capacity), slot, capacity)
    return slot.T, gates.T


def split3(val):
    hi = lax.reduce_precision(val, 8, 7)
    mid = lax.reduce_precision(val - hi, 8, 7)
    low = val - hi - mid
    return [part.astype(jnp.bfloat16) for part in (hi, mid, low)]


def moe_kernel(buf, wg, wu, wd, ret, xr, wgu_v, wd_v, x_v, o_v,
               w1s, w1r, w2s, w2r, w3s, w3r, lws, ds, dr, rs, rls, rr, xs, own):
    n_own = SIDE
    blk = wg.shape[1]
    n_src = xr.shape[1]
    half = x_v.shape[1]
    cap, d_model = buf.shape[1], buf.shape[2]
    d = lax.axis_index("data")
    p = lax.axis_index("expert")
    z, y = lax.div(d, SIDE), lax.rem(d, SIDE)
    x, c = lax.div(p, 2), lax.rem(p, 2)
    u = z * (1 - c) + y * c
    v = y * (1 - c) + z * c

    def data_of(uu, vv):
        return uu * (SIDE - 3 * c) + vv * (1 + 3 * c)

    v_up, v_dn = lax.rem(v + 1, SIDE), lax.rem(v + SIDE - 1, SIDE)

    def send(src, dst, s_sem, r_sem, data, expert):
        pltpu.make_async_remote_copy(src, dst, s_sem, r_sem, device_id={"data": data, "expert": expert}, device_id_type=MESH).start()

    def wait(ref, sem):
        pltpu.make_async_copy(ref, ref, sem).wait()

    def gu_block(e, b):
        return wgu_v.at[e, :, pl.ds(pl.multiple_of(b * blk, blk), blk), :]

    def gu_part(e, i, b):
        return wgu_v.at[e, i, pl.ds(pl.multiple_of(b * blk, blk), blk), :]

    def d_block(e, b):
        return wd_v.at[e, :, pl.ds(pl.multiple_of(b * blk, blk), blk)]

    def start_trade(e):
        own_e = n_own * u + e
        pltpu.make_async_copy(wg.at[own_e], gu_part(e, 0, d), lws.at[e, 0]).start()
        pltpu.make_async_copy(wu.at[own_e], gu_part(e, 1, d), lws.at[e, 1]).start()
        pltpu.make_async_copy(wd.at[own_e], d_block(e, d), lws.at[e, 2]).start()
        for r in range(1, SIDE):
            ut = lax.rem(u + r, SIDE)
            te = n_own * ut + e
            td = data_of(ut, v)
            send(wg.at[te], gu_part(e, 0, d), w1s.at[e, 0], w1r.at[e, 0], td, p)
            send(wu.at[te], gu_part(e, 1, d), w1s.at[e, 0], w1r.at[e, 0], td, p)
            send(wd.at[te], d_block(e, d), w1s.at[e, 1], w1r.at[e, 1], td, p)

    def start_rows(e):
        def body(k, carry):
            dx, cb, r = lax.div(k, 8), lax.rem(lax.div(k, SIDE), 2), lax.rem(k, SIDE)
            tx, tc = lax.rem(x + dx, SIDE), lax.rem(c + cb, 2)
            tz = lax.rem(z + r * (1 - tc), SIDE)
            ty = lax.rem(y + r * tc, SIDE)
            tp = tx * 2 + tc
            te = tp * (SIDE * n_own) + n_own * (tz * (1 - tc) + ty * tc) + e
            send(buf.at[te], xr.at[e, k], ds.at[e], dr.at[e], tz * SIDE + ty, tp)
            return carry

        lax.fori_loop(1, n_src, body, 0)

    def start_gather(e):
        pltpu.make_async_copy(wg.at[0], gu_part(e, 0, d), lws.at[e, 0]).wait()
        pltpu.make_async_copy(wu.at[0], gu_part(e, 1, d), lws.at[e, 1]).wait()
        pltpu.make_async_copy(wd.at[0], d_block(e, d), lws.at[e, 2]).wait()
        wait(wgu_v.at[e, :, pl.ds(0, 3 * blk), :], w1r.at[e, 0])
        wait(wd_v.at[e, :, pl.ds(0, 3 * blk)], w1r.at[e, 1])
        for i in range(SIDE):
            b = data_of(i, v)
            for vt in (v_up, v_dn):
                send(gu_block(e, b), gu_block(e, b), w2s.at[e, 0], w2r.at[e, 0], data_of(u, vt), p)
                send(d_block(e, b), d_block(e, b), w2s.at[e, 1], w2r.at[e, 1], data_of(u, vt), p)

    def start_relay(e):
        wait(wgu_v.at[e, :, pl.ds(0, 8 * blk), :], w2r.at[e, 0])
        wait(wd_v.at[e, :, pl.ds(0, 8 * blk)], w2r.at[e, 1])
        for i in range(SIDE):
            vs, vt = (v_dn, v_up) if i < SIDE // 2 else (v_up, v_dn)
            b = data_of(i, vs)
            send(gu_block(e, b), gu_block(e, b), w3s.at[e, 0], w3r.at[e, 0], data_of(u, vt), p)
            send(d_block(e, b), d_block(e, b), w3s.at[e, 1], w3r.at[e, 1], data_of(u, vt), p)

    def load(e, sb):
        return pltpu.make_async_copy(xr.at[e, pl.ds(sb * half, half)], x_v.at[sb], xs.at[sb])

    def experts(e, slot):
        wait(wgu_v.at[e, :, pl.ds(0, 4 * blk), :], w3r.at[e, 0])
        wait(wd_v.at[e, :, pl.ds(0, 4 * blk)], w3r.at[e, 1])
        wait(xr.at[e, pl.ds(1, n_src - 1)], dr.at[e])
        parts = n_src // half
        for sb in range(parts):
            load(e, sb).start()
        for sb in range(parts):
            load(e, sb).wait()
            rows = x_v[sb].reshape(half * cap, d_model)
            gate_pre = jnp.dot(rows, wgu_v[e, 0], preferred_element_type=jnp.float32)
            up_pre = jnp.dot(rows, wgu_v[e, 1], preferred_element_type=jnp.float32)
            hidden = (jax.nn.silu(gate_pre) * up_pre).astype(jnp.bfloat16)
            res = jnp.dot(hidden, wd_v[e], preferred_element_type=jnp.float32).astype(jnp.bfloat16)
            o_v[slot, pl.ds(sb * half, half)] = res.reshape(half, cap, d_model)
        my_e = p * (SIDE * n_own) + n_own * u + e

        def body(k, carry):
            dx, cb, r = lax.div(k, 8), lax.rem(lax.div(k, SIDE), 2), lax.rem(k, SIDE)
            sp = lax.rem(x + SIDE - dx, SIDE) * 2 + lax.rem(c + cb, 2)
            sd = data_of(lax.rem(u + SIDE - r, SIDE), v)
            send(o_v.at[slot, k], ret.at[my_e], rs.at[slot], rr, sd, sp)
            return carry

        lax.fori_loop(1, n_src, body, 0)
        pltpu.make_async_copy(o_v.at[slot, 0], ret.at[my_e], rls.at[slot]).start()

    def wait_results(slot):
        wait(o_v.at[slot, pl.ds(1, n_src - 1)], rs.at[slot])
        pltpu.make_async_copy(o_v.at[slot, 0], ret.at[0], rls.at[slot]).wait()

    def own_rows():
        return pltpu.make_async_copy(buf.at[pl.ds(p * (SIDE * n_own) + n_own * u, n_own)], xr.at[:, 0], own)

    own_rows().start()
    start_trade(0)
    start_rows(0)
    start_trade(1)
    start_rows(1)
    start_gather(0)
    start_trade(2)
    start_rows(2)
    start_relay(0)
    start_gather(1)
    start_trade(3)
    start_rows(3)
    own_rows().wait()

    def step(e, carry):
        slot = lax.rem(e, 2)

        @pl.when(e >= 2)
        def _():
            wait_results(slot)

        experts(e, slot)

        @pl.when(e + 1 < n_own)
        def _():
            start_relay(e + 1)

        @pl.when(e + 2 < n_own)
        def _():
            start_gather(e + 2)

        return carry

    lax.fori_loop(0, n_own, step, 0)
    for slot in range(2):
        wait_results(slot)
    wait(ret.at[pl.ds(0, n_own * (n_src - 1))], rr)

    def drain(e, carry):
        wait(wgu_v.at[e, :, pl.ds(0, 3 * blk), :], w1s.at[e, 0])
        wait(wd_v.at[e, :, pl.ds(0, 3 * blk)], w1s.at[e, 1])
        wait(wgu_v.at[e, :, pl.ds(0, 8 * blk), :], w2s.at[e, 0])
        wait(wd_v.at[e, :, pl.ds(0, 8 * blk)], w2s.at[e, 1])
        wait(wgu_v.at[e, :, pl.ds(0, 4 * blk), :], w3s.at[e, 0])
        wait(wd_v.at[e, :, pl.ds(0, 4 * blk)], w3s.at[e, 1])
        wait(xr.at[e, pl.ds(1, n_src - 1)], ds.at[e])
        return carry

    lax.fori_loop(0, n_own, drain, 0)


def moe(buffer, wg_loc, wu_loc, wd_loc):
    n_exp, cap, d_model = buffer.shape
    n_loc, blk, ff = wg_loc.shape
    n_own, n_src = SIDE, 8 * SIDE
    dma = pltpu.SemaphoreType.DMA
    bf16 = jnp.bfloat16
    any_spec = pl.BlockSpec(memory_space=pl.ANY)
    return pl.pallas_call(
        moe_kernel,
        out_shape=(jax.ShapeDtypeStruct(buffer.shape, bf16), jax.ShapeDtypeStruct((n_own, n_src, cap, d_model), bf16)),
        in_specs=[any_spec] * 4,
        out_specs=(any_spec, any_spec),
        scratch_shapes=[
            pltpu.VMEM((n_own, 2, d_model, ff), bf16),
            pltpu.VMEM((n_own, ff, d_model), bf16),
            pltpu.VMEM((2, n_src // 2, cap, d_model), bf16),
            pltpu.VMEM((2, n_src, cap, d_model), bf16),
        ] + [dma((n_own, 2))] * 6 + [dma((n_own, 3)), dma((n_own,)), dma((n_own,)), dma((2,)), dma((2,)), dma, dma((2,)), dma],
        compiler_params=pltpu.CompilerParams(has_side_effects=True, vmem_limit_bytes=64000 * 1024),
        cost_estimate=pl.CostEstimate(flops=6 * n_exp * cap * d_model * ff * 10, bytes_accessed=100_000_000, transcendentals=n_exp * cap * ff),
        name="moe_exchange",
    )(buffer, wg_loc, wu_loc, wd_loc)[0]


def solution(mesh):
    exp_n = mesh.shape["expert"]
    tok_spec = P(("rep", "expert", "data"), None)
    group_axes = ("expert", "data")

    def device_fn(x_loc, idx_loc, gate_loc, wg_loc, wu_loc, wd_loc, wsg_loc, wsu_loc, wsd_loc):
        tok_count, d_model = x_loc.shape
        n_exp = wg_loc.shape[0] * exp_n
        ff_shared = wsg_loc.shape[1]
        capacity = capacity_of(tok_count, idx_loc.shape[1], n_exp)
        ws_loc = jnp.concatenate([wsg_loc, wsu_loc, wsd_loc.T], axis=1)
        ws_all = lax.all_gather(ws_loc, group_axes, axis=0, tiled=True)
        slot, gates = routing(idx_loc, gate_loc, n_exp, capacity)
        sel = slot[:, None, :] == jnp.arange(capacity, dtype=jnp.int32)[None, :, None]
        pick = sel.astype(jnp.bfloat16).reshape(n_exp * capacity, tok_count)
        buffer = jnp.dot(pick, x_loc, preferred_element_type=jnp.float32).astype(jnp.bfloat16)
        returned = moe(buffer.reshape(n_exp, capacity, d_model), wg_loc, wu_loc, wd_loc)
        returned = returned.reshape(n_exp * capacity, d_model)
        s_gate = jnp.dot(x_loc, ws_all[:, :ff_shared], preferred_element_type=jnp.float32)
        s_up = jnp.dot(x_loc, ws_all[:, ff_shared:2 * ff_shared], preferred_element_type=jnp.float32)
        s_hidden = (jax.nn.silu(s_gate) * s_up).astype(jnp.bfloat16)
        total = lax.dot_general(s_hidden, ws_all[:, 2 * ff_shared:], (((1,), (1,)), ((), ())), preferred_element_type=jnp.float32)
        total += x_loc.astype(jnp.float32)
        for part in split3(gates):
            weight = jnp.where(sel, part[:, None, :], jnp.zeros((), jnp.bfloat16)).reshape(n_exp * capacity, tok_count)
            total += lax.dot_general(weight, returned, (((0,), (0,)), ((), ())), preferred_element_type=jnp.float32)
        return total.astype(jnp.bfloat16)

    in_specs = (tok_spec, tok_spec, tok_spec, P("expert", "data", None), P("expert", "data", None), P("expert", None, "data"), P(group_axes, None), P(group_axes, None), P(None, group_axes))
    return jax.shard_map(device_fn, mesh=mesh, in_specs=in_specs, out_specs=tok_spec, check_vma=False)
```

time: 715 us -> 543 us (0.76)
  waiting for transfers between devices: 505 us -> 0.02 us
  Pallas kernels: 0 us -> 448 us
  matrix products: 110 us -> 62.9 us
  blocking collectives: 45.6 us -> 0 us
  starting transfers between devices: 35.1 us -> 0.01 us
  local copies, waits for them, and re-layouts: 0.86 us -> 11.9 us
    pallas_call x0 -> x1, Pallas kernels: none -> 448 us  [moe(): pl.pallas_call(moe_kernel, out_shape=(jax.ShapeDtypeStruct(buffer.shape,...]
    all_to_all x4 -> x0, waiting for transfers between devices: 271 us -> none  [the longest x1 232 us: device_fn(): lax.all_to_all(buffer.reshape(n_exp, capacity, d_model), group_axes, 0, 0...]
    all_gather x3 -> x1, waiting for transfers between devices: 231 us -> 0.01 us  [device_fn(): ws_all = lax.all_gather(ws_loc, group_axes, axis=0, tiled=True)]
    dot_general x4 -> x2, matrix products: 63.9 us -> 12.6 us  [the longest x1 8.86 us: device_fn(): lax.dot_general(s_hidden, ws_all[:, 2 * ff_shared:], (((1,), (1,)), ((),...]
    all_to_all x1 -> x0, blocking collectives: 45.6 us -> none  [device_fn(): lax.all_to_all(wg_loc, 'data', 0, 1, tiled=True).reshape(d_model, ff)]
    all_to_all x4 -> x0, starting transfers between devices: 34.7 us -> none  [the longest x1 15.9 us: device_fn(): lax.all_to_all(expert_out.reshape(n_exp, capacity, d_model), group_axes,...]
    unnamed x10 -> x20, local copies, waits for them, and re-layouts: 0.26 us -> 9.84 us
  transfers between devices with their start and end apart: 7 -> 1, of which waited for: 5 -> 0; matrix products, arithmetic and copies ran while one was open for 12% -> 9% of each run, Pallas kernels for 0% -> 83%
where the time goes in v2:
time: 543 us; the launch traced here: 541 us
  Pallas kernels  448 us (83%)
  matrix products  62.9 us (12%)
  between operations  13.6 us (3%)
  local copies, waits for them, and re-layouts  11.9 us (2%)
    pallas_call x1, Pallas kernels, moe(): pl.pallas_call(moe_kernel, out_shape=(jax.ShapeDtypeStruct(buffer.shape,...  448 us
    dot_general x3, matrix products, device_fn(): lax.dot_general(weight, returned, (((0,), (0,)), ((), ())), preferred_ele...  36.3 us
    dot_general x1, matrix products, device_fn(): jnp.dot(pick, x_loc, preferred_element_type=jnp.float32)  13.7 us
  transfers between devices with their start and end apart: 1, of which 0 were waited for; matrix products, arithmetic and copies ran while one was open for 9% of the time, Pallas kernels for 83%

profile of v2, /device:TPU:1, one launch (start us, length us, event | category | flops | bytes accessed | tf_op | source)
XLA Modules:
  0.0 540.9 jit_solution(4528334498330658669)
XLA Ops:
  6.5 1.5 concatenate.3
  8.1 0.8 copy.28
  8.9 0.7 copy-done.1
  9.6 2.0 fusion.27
  11.6 0.1 copy.29
  11.8 0.1 eq.45
  11.9 4.7 copy.32.wg
  16.6 2.8 copy.33.wu
  19.4 0.3 fusion.50
  19.7 0.7 copy-done.3
  20.4 1.0 bitcast_compare_fusion
  21.4 13.7 %convolution_convert_fusion = bf16[4096,2048]{1,0:T(8,128)(2,1)} fusion(pred[4096,384]{1,0:T(32,128)(4,1)S(1)} %bitcast_compare_fusion, bf16[384,2048]{1,0:T(8,128)(2,1)} %param.9), kind=kOutput, calls=%fused_computation | convolution fusion | flops 6450839552 | bytes 19922944 | tf_op jit(solution)/shard_map/dot_general | solution.py:244
  35.1 447.6 %moe_exchange.1 = (bf16[128,32,2048]{2,1,0:T(8,128)(2,1)}, bf16[4,32,32,2048]{3,2,1,0:T(8,128)(2,1)}) custom-call(bf16[128,32,2048]{2,1,0:T(8,128)(2,1)} %bitcast.45, bf16[16,128,704]{2,1,0:T(8,128)(2,1)} %copy.32.wg, bf16[16,128,704]{2,1,0:T(8,128)(2,1)} %copy.33.wu, bf16[16,704,128]{2,1,0:T(8,128)(2,1)} %wd.1), custom_call_target="tpu_custom_call" | custom-call | flops 354334801920 | bytes 100000000 | tf_op jit(solution)/shard_map/moe_exchange/pallas_call | solution.py:212
  482.7 0.1 copy.30
  482.8 1.9 select_reduce_fusion
  484.7 0.1 fusion.49
  484.8 0.1 copy.31
  484.9 0.1 copy.34
  485.0 0.1 copy.35
  485.2 12.3 %fusion.3 = f32[384,2048,1]{1,0,2:T(8,128)} fusion(bf16[128,32,2048]{2,1,0:T(8,128)(2,1)} %get-tuple-element.6, s32[128,384]{1,0:T(8,128)S(1)} %copy-done.4, bf16[128,384]{1,0:T(8,128)(2,1)S(1)} %copy.31), kind=kOutput, calls=%fused_computation.6 | convolution fusion | flops 6445596672 | bytes 20217856 | tf_op jit(solution)/shard_map/dot_general | solution.py:254
  497.5 8.8 %fusion.5 = f32[384,2048,1]{1,0,2:T(8,128)} fusion(bf16[128,32,2048]{2,1,0:T(8,128)(2,1)S(1)} %copy-done.7, s32[128,384]{1,0:T(8,128)S(1)} %copy-done.4, bf16[128,384]{1,0:T(8,128)(2,1)S(1)} %copy.34), kind=kOutput, calls=%fused_computation.7 | convolution fusion | flops 6445596672 | bytes 20217856 | tf_op jit(solution)/shard_map/dot_general | solution.py:254
  506.2 3.7 fusion.28
  510.0 8.9 %fusion.9 = f32[384,2048]{1,0:T(8,128)} fusion(bf16[2048,2112]{1,0:T(8,128)(2,1)} %all-gather.2.cloned.1.call-done, bf16[384,2048]{1,0:T(8,128)(2,1)S(1)} %copy-done.6, f32[384,704]{0,1:T(8,128)S(1)} %fusion.28), kind=kOutput, calls=%fused_computation.9 | convolution fusion | flops 2216214528 | bytes 12091392 | tf_op jit(solution)/shard_map/dot_general | solution.py:250
  518.8 15.3 %fusion.15 = bf16[384,2048]{1,0:T(8,128)(2,1)} fusion(f32[384,2048,1]{1,0,2:T(8,128)} %fusion.5, f32[384,2048,1]{1,0,2:T(8,128)} %fusion.3, f32[384,2048]{1,0:T(8,128)} %fusion.9, bf16[384,2048]{1,0:T(8,128)(2,1)S(1)} %copy-done.6, bf16[128,32,2048]{2,1,0:T(8,128)(2,1)} %get-tuple-element.6, s32[128,384]{1,0:T(8,128)S(1)} %copy-done.4, ...), kind=kOutput, calls=%fused_computation.16 | convolution fusion | flops 6450315264 | bytes 29655040 | tf_op jit(solution)/shard_map/dot_general | solution.py:254
  (19 shorter events, 0.1 us)
Async XLA Ops:
  6.5 499.7 %all-gather.2.cloned.1.call-start = ((), (), s32[]{:S(2)}) async-start(), calls=%async_computation | async-start | bytes 8982528 | tf_op jit(solution)/shard_map/all_gather | solution.py:240
  8.9 0.7 copy-start.1
  11.6 5.0 copy-start
  19.7 0.7 copy-start.3
  35.1 447.6 %copy-start.5 = (f32[384,8]{0,1:T(8,128)S(1)}, f32[384,8]{0,1:T(8,128)}, u32[]{:S(2)}) copy-start(f32[384,8]{0,1:T(8,128)} %param.11) | copy-start | bytes 36868
  35.1 447.7 %copy-start.2 = (s32[384,8]{1,0:T(8,128)S(1)}, s32[384,8]{1,0:T(8,128)}, u32[]{:S(2)}) copy-start(s32[384,8]{1,0:T(8,128)} %copy-done.1) | copy-start | bytes 36868
  35.1 450.1 %copy-start.4 = (s32[128,384]{1,0:T(8,128)S(1)}, s32[128,384]{1,0:T(8,128)}, u32[]{:S(2)}) copy-start(s32[128,384]{1,0:T(8,128)} %copy-done.3) | copy-start | bytes 589828
  485.2 12.3 %copy-start.7 = (bf16[128,32,2048]{2,1,0:T(8,128)(2,1)S(1)}, bf16[128,32,2048]{2,1,0:T(8,128)(2,1)}, u32[]{:S(2)}) copy-start(bf16[128,32,2048]{2,1,0:T(8,128)(2,1)} %get-tuple-element.6) | copy-start | bytes 50331652
  497.5 8.8 %copy-start.6 = (bf16[384,2048]{1,0:T(8,128)(2,1)S(1)}, bf16[384,2048]{1,0:T(8,128)(2,1)}, u32[]{:S(2)}) copy-start(bf16[384,2048]{1,0:T(8,128)(2,1)} %param.9) | copy-start | bytes 4718596
Sparse Core Ops, SparseCore 0:
  10.5 155.3 all-gather.1

commit v3 on v1

v3 whole, which is shorter than its diff:
```python
import jax
import jax.numpy as jnp
from jax import lax
from jax.experimental import pallas as pl
from jax.experimental.pallas import tpu as pltpu
from jax.sharding import PartitionSpec as P

MESH = pl.DeviceIdType.MESH
CAP_NUM = 5
CAP_DEN = 4
SIDE = 4


def capacity_of(tok_count, top_count, n_exp):
    return max(8, ((CAP_NUM * top_count * tok_count) // (CAP_DEN * n_exp) + 7) // 8 * 8)


def routing(idx_loc, gate_loc, n_exp, capacity):
    tok_count = idx_loc.shape[0]
    hit = idx_loc[:, :, None] == jnp.arange(n_exp, dtype=jnp.int32)[None, None, :]
    chosen = jnp.any(hit, axis=1)
    gates = jnp.sum(jnp.where(hit, gate_loc[:, :, None], 0.0), axis=1)
    before = jnp.tril(jnp.ones((tok_count, tok_count), jnp.bfloat16), -1)
    slot = jnp.dot(before, chosen.astype(jnp.bfloat16), preferred_element_type=jnp.float32).astype(jnp.int32)
    slot = jnp.where(chosen & (slot < capacity), slot, capacity)
    return slot.T, gates.T


def moe_kernel(x_in, slot_in, gate_in, wg, wu, wd, acc, xr, ret, w_v, pool, x_v, t_v,
               w1s, w1r, w2s, w2r, w3s, w3r, lws, ds, dr, rs, rls, rr, xs, own):
    n_own = SIDE
    blk = wg.shape[2]
    n_src, cap, d_model = xr.shape[1:]
    tok_count = x_in.shape[0]
    unit = x_v.shape[1]
    units = n_src // unit
    d = lax.axis_index("data")
    p = lax.axis_index("expert")
    z, y = lax.div(d, SIDE), lax.rem(d, SIDE)
    x, c = lax.div(p, 2), lax.rem(p, 2)
    u = z * (1 - c) + y * c
    v = y * (1 - c) + z * c
    v_up, v_dn = lax.rem(v + 1, SIDE), lax.rem(v + SIDE - 1, SIDE)
    slots = lax.broadcasted_iota(jnp.int32, (cap, tok_count), 0)

    def data_of(uu, vv):
        return uu * (SIDE - 3 * c) + vv * (1 + 3 * c)

    def target(k):
        dx, cb, r = lax.div(k, 8), lax.rem(lax.div(k, SIDE), 2), lax.rem(k, SIDE)
        tx, tc = lax.rem(x + dx, SIDE), lax.rem(c + cb, 2)
        tz = lax.rem(z + r * (1 - tc), SIDE)
        ty = lax.rem(y + r * tc, SIDE)
        tp = tx * 2 + tc
        return tp, tz * SIDE + ty, tp * (SIDE * n_own) + n_own * (tz * (1 - tc) + ty * tc)

    def source(k):
        dx, cb, r = lax.div(k, 8), lax.rem(lax.div(k, SIDE), 2), lax.rem(k, SIDE)
        sp = lax.rem(x + SIDE - dx, SIDE) * 2 + lax.rem(c + cb, 2)
        return sp, data_of(lax.rem(u + SIDE - r, SIDE), v)

    def send(src, dst, s_sem, r_sem, data, expert):
        pltpu.make_async_remote_copy(src, dst, s_sem, r_sem, device_id={"data": data, "expert": expert}, device_id_type=MESH).start()

    def wait(ref, sem):
        pltpu.make_async_copy(ref, ref, sem).wait()

    def strips(e, count):
        return w_v.at[e, :, :, pl.ds(0, count * blk)]

    def strip(e, b):
        return w_v.at[e, :, :, pl.ds(pl.multiple_of(b * blk, blk), blk)]

    def part(e, i, b):
        return w_v.at[e, i, :, pl.ds(pl.multiple_of(b * blk, blk), blk)]

    def start_trade(e):
        for i, w in enumerate((wg, wu, wd)):
            pltpu.make_async_copy(w.at[n_own * u + e], part(e, i, d), lws.at[e, i]).start()
        for r in range(1, SIDE):
            ut = lax.rem(u + r, SIDE)
            for i, w in enumerate((wg, wu, wd)):
                send(w.at[n_own * ut + e], part(e, i, d), w1s.at[e], w1r.at[e], data_of(ut, v), p)

    def start_rows(e, slot):
        def pick(g, carry):
            for j in range(unit):
                te = target(g * unit + j)[2] + e
                t_v[0, j * cap:(j + 1) * cap, :] = (slots == slot_in[pl.ds(te, 1), :]).astype(jnp.bfloat16)
            rows = jnp.dot(t_v[0], x_in[...], preferred_element_type=jnp.float32).astype(jnp.bfloat16)
            pool[slot, pl.ds(g * unit, unit)] = rows.reshape(unit, cap, d_model)
            return carry

        lax.fori_loop(0, units, pick, 0)

        def body(k, carry):
            tp, td, _ = target(k)
            send(pool.at[slot, k], xr.at[e, k], ds.at[e], dr.at[e], td, tp)
            return carry

        lax.fori_loop(1, n_src, body, 0)
        pltpu.make_async_copy(pool.at[slot, 0], xr.at[e, 0], own.at[e]).start()

    def wait_rows_sent(e, slot):
        wait(pool.at[slot, pl.ds(1, n_src - 1)], ds.at[e])
        pltpu.make_async_copy(pool.at[slot, 0], xr.at[e, 0], own.at[e]).wait()

    def start_gather(e):
        for i, w in enumerate((wg, wu, wd)):
            pltpu.make_async_copy(w.at[0], part(e, i, d), lws.at[e, i]).wait()
        wait(strips(e, 3), w1r.at[e])
        for i in range(SIDE):
            b = data_of(i, v)
            for vt in (v_up, v_dn):
                send(strip(e, b), strip(e, b), w2s.at[e], w2r.at[e], data_of(u, vt), p)

    def start_relay(e):
        wait(strips(e, 8), w2r.at[e])
        for i in range(SIDE):
            vs, vt = (v_dn, v_up) if i < SIDE // 2 else (v_up, v_dn)
            b = data_of(i, vs)
            send(strip(e, b), strip(e, b), w3s.at[e], w3r.at[e], data_of(u, vt), p)

    def load(src, e, g, s):
        return pltpu.make_async_copy(src.at[e, pl.ds(g * unit, unit)], x_v.at[s], xs.at[s])

    def streamed(src, e, work):
        load(src, e, 0, 0).start()

        def body(g, carry):
            s = lax.rem(g, 2)

            @pl.when(g + 1 < units)
            def _():
                load(src, e, g + 1, 1 - s).start()

            load(src, e, g, s).wait()
            work(g, x_v[s].reshape(unit * cap, d_model))
            return carry

        lax.fori_loop(0, units, body, 0)

    def give_back(e, slot, k):
        sp, sd = source(k)
        send(pool.at[slot, k], ret.at[e, k], rs.at[e], rr.at[e], sd, sp)

    def experts(e, slot):
        wait(strips(e, 4), w3r.at[e])
        wait(xr.at[e, pl.ds(1, n_src - 1)], dr.at[e])
        nt = (((1,), (1,)), ((), ()))

        def send_unit(g):
            for j in range(unit):
                give_back(e, slot, g * unit + j)

        def work(g, rows):
            gate_pre = lax.dot_general(rows, w_v[e, 0], nt, preferred_element_type=jnp.float32)
            up_pre = lax.dot_general(rows, w_v[e, 1], nt, preferred_element_type=jnp.float32)
            hidden = (jax.nn.silu(gate_pre) * up_pre).astype(jnp.bfloat16)
            res = jnp.dot(hidden, w_v[e, 2], preferred_element_type=jnp.float32).astype(jnp.bfloat16)
            pool[slot, pl.ds(g * unit, unit)] = res.reshape(unit, cap, d_model)

            @pl.when(g == 1)
            def _():
                for j in range(1, unit):
                    give_back(e, slot, j)

            @pl.when(g > 1)
            def _():
                send_unit(g - 1)

        streamed(xr, e, work)
        send_unit(units - 1)
        pltpu.make_async_copy(pool.at[slot, 0], ret.at[e, 0], rls.at[e]).start()

    def wait_results_sent(e, slot):
        wait(pool.at[slot, pl.ds(1, n_src - 1)], rs.at[e])

    def combine(e):
        wait(ret.at[e, pl.ds(1, n_src - 1)], rr.at[e])
        pltpu.make_async_copy(pool.at[0, 0], ret.at[e, 0], rls.at[e]).wait()
        tn = (((0,), (0,)), ((), ()))
        width = d_model // 4

        def work(g, rows):
            for j in range(unit):
                te = target(g * unit + j)[2] + e
                val = jnp.where(slots == slot_in[pl.ds(te, 1), :], gate_in[pl.ds(te, 1), :], 0.0)
                hi = val.astype(jnp.bfloat16)
                rest = val - hi.astype(jnp.float32)
                mid = rest.astype(jnp.bfloat16)
                low = (rest - mid.astype(jnp.float32)).astype(jnp.bfloat16)
                for i, term in enumerate((hi, mid, low)):
                    t_v[i, j * cap:(j + 1) * cap, :] = term
            for n in range(4):
                cols = rows[:, n * width:(n + 1) * width]
                total = acc[:, n * width:(n + 1) * width]
                for i in range(3):
                    total += lax.dot_general(t_v[i], cols, tn, preferred_element_type=jnp.float32)
                acc[:, n * width:(n + 1) * width] = total

        streamed(ret, e, work)

    start_trade(0)
    start_rows(0, 0)
    start_trade(1)
    start_rows(1, 1)
    acc[...] = jnp.zeros_like(acc)
    start_gather(0)
    start_trade(2)
    start_rows(2, 2)
    start_relay(0)
    start_gather(1)
    start_trade(3)
    wait_rows_sent(0, 0)
    start_rows(3, 0)

    def step(e, carry):
        slot = lax.rem(e + 1, 3)

        @pl.when(e < 3)
        def _():
            wait_rows_sent(e + 1, slot)

        @pl.when(e == 3)
        def _():
            wait_results_sent(0, 1)

        experts(e, slot)

        @pl.when(e + 1 < n_own)
        def _():
            start_relay(e + 1)

        @pl.when(e + 2 < n_own)
        def _():
            start_gather(e + 2)

        @pl.when(e >= 1)
        def _():
            combine(e - 1)

        return carry

    lax.fori_loop(0, n_own, step, 0)
    for e in range(1, n_own):
        wait_results_sent(e, (e + 1) % 3)
    combine(n_own - 1)

    def drain(e, carry):
        wait(strips(e, 3), w1s.at[e])
        wait(strips(e, 8), w2s.at[e])
        wait(strips(e, 4), w3s.at[e])
        return carry

    lax.fori_loop(0, n_own, drain, 0)


def moe(x_loc, slot, gates, wg_loc, wu_loc, wd_loc, cap):
    tok_count, d_model = x_loc.shape
    n_loc, blk, ff = wg_loc.shape
    n_exp = slot.shape[0]
    n_own, n_src, unit = SIDE, 8 * SIDE, 8
    dma = pltpu.SemaphoreType.DMA
    bf16 = jnp.bfloat16
    any_spec = pl.BlockSpec(memory_space=pl.ANY)
    vmem_spec = pl.BlockSpec(memory_space=pltpu.VMEM)
    stage = jax.ShapeDtypeStruct((n_own, n_src, cap, d_model), bf16)
    return pl.pallas_call(
        moe_kernel,
        out_shape=(jax.ShapeDtypeStruct((tok_count, d_model), jnp.float32), stage, stage),
        in_specs=[vmem_spec] * 3 + [any_spec] * 3,
        out_specs=(vmem_spec, any_spec, any_spec),
        scratch_shapes=[
            pltpu.VMEM((n_own, 3, ff, d_model), bf16),
            pltpu.VMEM((3, n_src, cap, d_model), bf16),
            pltpu.VMEM((2, unit, cap, d_model), bf16),
            pltpu.VMEM((3, unit * cap, tok_count), bf16),
        ] + [dma((n_own,))] * 6 + [dma((n_own, 3))] + [dma((n_own,))] * 5 + [dma((2,)), dma((n_own,))],
        compiler_params=pltpu.CompilerParams(has_side_effects=True, vmem_limit_bytes=65400 * 1024),
        cost_estimate=pl.CostEstimate(flops=60 * n_exp * cap * d_model * ff, bytes_accessed=100_000_000, transcendentals=n_exp * cap * ff),
        name="moe_exchange",
    )(x_loc, slot, gates, jnp.swapaxes(wg_loc, 1, 2), jnp.swapaxes(wu_loc, 1, 2), wd_loc)[0]


def solution(mesh):
    exp_n = mesh.shape["expert"]
    tok_spec = P(("rep", "expert", "data"), None)
    group_axes = ("expert", "data")

    def device_fn(x_loc, idx_loc, gate_loc, wg_loc, wu_loc, wd_loc, wsg_loc, wsu_loc, wsd_loc):
        tok_count, d_model = x_loc.shape
        n_exp = wg_loc.shape[0] * exp_n
        ff_shared = wsg_loc.shape[1]
        capacity = capacity_of(tok_count, idx_loc.shape[1], n_exp)
        ws_loc = jnp.concatenate([wsg_loc, wsu_loc, wsd_loc.T], axis=1)
        ws_all = lax.all_gather(ws_loc, group_axes, axis=0, tiled=True)
        slot, gates = routing(idx_loc, gate_loc, n_exp, capacity)
        routed = moe(x_loc, slot, gates, wg_loc, wu_loc, wd_loc, capacity)
        pre = jnp.dot(x_loc, ws_all[:, :2 * ff_shared], preferred_element_type=jnp.float32)
        s_hidden = (jax.nn.silu(pre[:, :ff_shared]) * pre[:, ff_shared:]).astype(jnp.bfloat16)
        shared = lax.dot_general(s_hidden, ws_all[:, 2 * ff_shared:], (((1,), (1,)), ((), ())), preferred_element_type=jnp.float32)
        return (x_loc.astype(jnp.float32) + shared + routed).astype(jnp.bfloat16)

    in_specs = (tok_spec, tok_spec, tok_spec, P("expert", "data", None), P("expert", "data", None), P("expert", None, "data"), P(group_axes, None), P(group_axes, None), P(None, group_axes))
    return jax.shard_map(device_fn, mesh=mesh, in_specs=in_specs, out_specs=tok_spec, check_vma=False)
```

time: 715 us -> 483 us (0.68)
  waiting for transfers between devices: 505 us -> 0.04 us
  Pallas kernels: 0 us -> 449 us
  matrix products: 110 us -> 12.1 us
  blocking collectives: 45.6 us -> 0 us
  starting transfers between devices: 35.1 us -> 0.01 us
    pallas_call x0 -> x1, Pallas kernels: none -> 449 us  [moe(): pl.pallas_call(moe_kernel, out_shape=(jax.ShapeDtypeStruct((tok_count, d_...]
    all_to_all x4 -> x0, waiting for transfers between devices: 271 us -> none  [the longest x1 232 us: device_fn(): lax.all_to_all(buffer.reshape(n_exp, capacity, d_model), group_axes, 0, 0...]
    all_gather x3 -> x1, waiting for transfers between devices: 231 us -> 0.02 us  [device_fn(): ws_all = lax.all_gather(ws_loc, group_axes, axis=0, tiled=True)]
    dot_general x8 -> x2, matrix products: 110 us -> 11.1 us  [the longest x1 6.5 us: device_fn(): jnp.dot(x_loc, ws_all[:, :2 * ff_shared], preferred_element_type=jnp.floa...]
    all_to_all x1 -> x0, blocking collectives: 45.6 us -> none  [device_fn(): lax.all_to_all(wg_loc, 'data', 0, 1, tiled=True).reshape(d_model, ff)]
    all_to_all x4 -> x0, starting transfers between devices: 34.7 us -> none  [the longest x1 15.9 us: device_fn(): lax.all_to_all(expert_out.reshape(n_exp, capacity, d_model), group_axes,...]
  transfers between devices with their start and end apart: 7 -> 1, of which waited for: 5 -> 0; matrix products, arithmetic and copies ran while one was open for 12% -> 2% of each run, Pallas kernels for 0% -> 93%
where the time goes in v3:
time: 483 us
  Pallas kernels  449 us (93%)
  between operations  13.5 us (3%)
  matrix products  12.1 us (3%)
    pallas_call x1, Pallas kernels, moe(): pl.pallas_call(moe_kernel, out_shape=(jax.ShapeDtypeStruct((tok_count, d_...  449 us
  transfers between devices with their start and end apart: 1, of which 0 were waited for; matrix products, arithmetic and copies ran while one was open for 2% of the time, Pallas kernels for 93%

profile of v3, /device:TPU:1, one launch (start us, length us, event | category | flops | bytes accessed | tf_op | source)
XLA Modules:
  0.0 482.8 jit_solution(17504074076816250117)
XLA Ops:
  6.5 0.0 all-gather.2.cloned.1.call-start
  6.5 1.5 concatenate.3
  8.0 0.0 all-gather.2.cloned.1.call-update
  8.1 0.8 copy.12
  8.9 2.0 fusion.9
  11.0 0.1 copy.13
  11.1 0.8 copy.14
  11.9 1.9 select_reduce_fusion
  13.8 0.8 copy.15
  14.6 1.0 fusion.16.slot_in
  15.6 449.2 %moe_exchange.1 = (f32[384,2048]{1,0:T(8,128)}, bf16[4,32,32,2048]{3,2,1,0:T(8,128)(2,1)}, bf16[4,32,32,2048]{3,2,1,0:T(8,128)(2,1)}) custom-call(bf16[384,2048]{1,0:T(8,128)(2,1)} %x_in.1, s32[128,384]{1,0:T(8,128)} %fusion.16.slot_in, f32[128,384]{1,0:T(8,128)} %bitcast.11, bf16[16,704,128]{2,1,0:T(8,128)(2,1)} %bitcast.13, ...), custom_call_target="tpu_custom_call" | custom-call | flops 354334801920 | bytes 100000000 | tf_op jit(solution)/shard_map/moe_exchange/pallas_call | solution.py:269
  464.8 0.0 copy-start
  464.8 0.0 all-gather.2.cloned.1.call-done
  464.9 0.0 copy-start.1
  464.9 6.5 %fusion.4 = f32[384,1408]{0,1:T(8,128)S(1)} fusion(bf16[384,2048]{1,0:T(8,128)(2,1)} %x_in.1, bf16[2048,2112]{1,0:T(8,128)(2,1)} %all-gather.2.cloned.1.call-done), kind=kOutput, calls=%fused_computation.5 | convolution fusion | flops 2214592512 | bytes 9502720 | tf_op jit(solution)/shard_map/dot_general | solution.py:300
  471.4 0.0 copy-done
  471.4 0.0 copy-done.1
  471.4 4.6 add_convert_fusion
  (1 shorter events, 0.0 us)
Async XLA Ops:
  6.5 458.3 %all-gather.2.cloned.1.call-start = ((), (), s32[]{:S(2)}) async-start(), calls=%async_computation | async-start | bytes 8982528 | tf_op jit(solution)/shard_map/all_gather | solution.py:297
  464.8 6.6 %copy-start = (bf16[384,2048]{1,0:T(8,128)(2,1)S(1)}, bf16[384,2048]{1,0:T(8,128)(2,1)}, u32[]{:S(2)}) copy-start(bf16[384,2048]{1,0:T(8,128)(2,1)} %x_in.1) | copy-start | bytes 4718596
  464.9 6.5 %copy-start.1 = (f32[384,2048]{1,0:T(8,128)S(1)}, f32[384,2048]{1,0:T(8,128)}, u32[]{:S(2)}) copy-start(f32[384,2048]{1,0:T(8,128)} %get-tuple-element.6) | copy-start | bytes 9437188
Sparse Core Ops, SparseCore 0:
  10.5 161.2 all-gather.1

commit v4 on v3

--- a/solution.py
+++ b/solution.py
@@ -6,6 +6,7 @@
 from jax.sharding import PartitionSpec as P
 
 MESH = pl.DeviceIdType.MESH
+OWN = 24
 CAP_NUM = 5
 CAP_DEN = 4
 SIDE = 4
@@ -26,8 +27,8 @@
     return slot.T, gates.T
 
 
-def moe_kernel(x_in, slot_in, gate_in, wg, wu, wd, acc, xr, ret, w_v, pool, x_v, t_v,
-               w1s, w1r, w2s, w2r, w3s, w3r, lws, ds, dr, rs, rls, rr, xs, own):
+def moe_kernel(x_in, slot_in, gate_in, ws_in, wg, wu, wd, acc, xr, ret, ws, w_v, pool, x_v, t_v, s_v, pre, h_v,
+               w1s, w1r, w2s, w2r, w3s, w3r, lws, ds, dr, rs, rls, rr, xs, own, ss, sr, sl, sx):
     n_own = SIDE
     blk = wg.shape[2]
     n_src, cap, d_model = xr.shape[1:]
@@ -47,7 +48,7 @@
         return uu * (SIDE - 3 * c) + vv * (1 + 3 * c)
 
     def target(k):
-        dx, cb, r = lax.div(k, 8), lax.rem(lax.div(k, SIDE), 2), lax.rem(k, SIDE)
+        dx, cb, r = lax.rem(lax.div(k, 8) + 1, SIDE), lax.rem(lax.div(k, SIDE), 2), lax.rem(k, SIDE)
         tx, tc = lax.rem(x + dx, SIDE), lax.rem(c + cb, 2)
         tz = lax.rem(z + r * (1 - tc), SIDE)
         ty = lax.rem(y + r * tc, SIDE)
@@ -55,7 +56,7 @@
         return tp, tz * SIDE + ty, tp * (SIDE * n_own) + n_own * (tz * (1 - tc) + ty * tc)
 
     def source(k):
-        dx, cb, r = lax.div(k, 8), lax.rem(lax.div(k, SIDE), 2), lax.rem(k, SIDE)
+        dx, cb, r = lax.rem(lax.div(k, 8) + 1, SIDE), lax.rem(lax.div(k, SIDE), 2), lax.rem(k, SIDE)
         sp = lax.rem(x + SIDE - dx, SIDE) * 2 + lax.rem(c + cb, 2)
         return sp, data_of(lax.rem(u + SIDE - r, SIDE), v)
 
@@ -73,6 +74,69 @@
 
     def part(e, i, b):
         return w_v.at[e, i, :, pl.ds(pl.multiple_of(b * blk, blk), blk)]
+
+    def shared_own():
+        return pltpu.make_async_copy(ws_in, ws.at[x, c, z, y], sl)
+
+    def shared_sent(s, sem):
+        wait((ws.at[0, 0, 0, pl.ds(0, 3)], ws.at[0, 0, pl.ds(0, 3)], ws.at[pl.ds(0, 3), 0], ws.at[:, 0])[s], sem.at[s])
+
+    def shared_stage(s):
+        if s == 0:
+            shared_own().start()
+            shared_own().wait()
+        else:
+            shared_sent(s - 1, sr)
+        if s == 3:
+            for core in range(2):
+                @pl.when(c == core)
+                def _(core=core):
+                    send(ws.at[:, core], ws.at[:, core], ss.at[s], sr.at[s], d, p + 1 - 2 * core)
+            return
+        ref = (ws.at[x, c, z, y], ws.at[x, c, z], ws.at[x, c])[s]
+        for r in range(1, SIDE):
+            ty = lax.rem(y + r, SIDE) if s == 0 else y
+            tz = lax.rem(z + r, SIDE) if s == 1 else z
+            tx = lax.rem(x + r, SIDE) if s == 2 else x
+            send(ref, ref, ss.at[s], sr.at[s], tz * SIDE + ty, tx * 2 + c)
+
+    def shared_expert():
+        shared_sent(3, sr)
+        wide = h_v.shape[1]
+        rows = s_v.shape[1] * s_v.shape[2] * s_v.shape[3]
+        planes = d_model // rows
+        nt = (((1,), (1,)), ((), ()))
+
+        def fetch(g, s):
+            return pltpu.make_async_copy(ws.at[lax.div(g, 2), lax.rem(g, 2)], s_v.at[s], sx.at[s])
+
+        def over_planes(work):
+            fetch(0, 0).start()
+
+            def body(g, carry):
+                s = lax.rem(g, 2)
+
+                @pl.when(g + 1 < planes)
+                def _():
+                    fetch(g + 1, 1 - s).start()
+
+                fetch(g, s).wait()
+                work(g, pl.ds(pl.multiple_of(g * rows, rows), rows), s_v[s].reshape(rows, 3 * wide))
+                return carry
+
+            lax.fori_loop(0, planes, body, 0)
+
+        pre[...] = jnp.zeros_like(pre)
+
+        def gate_up(g, cols, blkw):
+            pre[...] += jnp.dot(x_in[:, cols], blkw[:, :2 * wide], preferred_element_type=jnp.float32)
+
+        def down(g, cols, blkw):
+            acc[:, cols] += lax.dot_general(h_v[...], blkw[:, 2 * wide:], nt, preferred_element_type=jnp.float32)
+
+        over_planes(gate_up)
+        h_v[...] = (jax.nn.silu(pre[:, :wide]) * pre[:, wide:]).astype(jnp.bfloat16)
+        over_planes(down)
 
     def start_trade(e):
         for i, w in enumerate((wg, wu, wd)):
@@ -93,17 +157,18 @@
 
         lax.fori_loop(0, units, pick, 0)
 
-        def body(k, carry):
+        def body(i, carry):
+            k = i + lax.div(i, OWN)
             tp, td, _ = target(k)
             send(pool.at[slot, k], xr.at[e, k], ds.at[e], dr.at[e], td, tp)
             return carry
 
-        lax.fori_loop(1, n_src, body, 0)
-        pltpu.make_async_copy(pool.at[slot, 0], xr.at[e, 0], own.at[e]).start()
+        lax.fori_loop(0, n_src - 1, body, 0)
+        pltpu.make_async_copy(pool.at[slot, OWN], xr.at[e, OWN], own.at[e]).start()
 
     def wait_rows_sent(e, slot):
-        wait(pool.at[slot, pl.ds(1, n_src - 1)], ds.at[e])
-        pltpu.make_async_copy(pool.at[slot, 0], xr.at[e, 0], own.at[e]).wait()
+        wait(pool.at[slot, pl.ds(0, n_src - 1)], ds.at[e])
+        pltpu.make_async_copy(pool.at[slot, OWN], xr.at[e, OWN], own.at[e]).wait()
 
     def start_gather(e):
         for i, w in enumerate((wg, wu, wd)):
@@ -124,6 +189,17 @@
     def load(src, e, g, s):
         return pltpu.make_async_copy(src.at[e, pl.ds(g * unit, unit)], x_v.at[s], xs.at[s])
 
+    def arrived(src, e, work, landed):
+        def body(i, carry):
+            s, g = lax.rem(i, 2), lax.rem(i + 3, units)
+            landed(g)
+            load(src, e, g, s).start()
+            load(src, e, g, s).wait()
+            work(g, x_v[s].reshape(unit * cap, d_model))
+            return carry
+
+        lax.fori_loop(0, units, body, 0)
+
     def streamed(src, e, work):
         load(src, e, 0, 0).start()
 
@@ -142,15 +218,15 @@
 
     def give_back(e, slot, k):
         sp, sd = source(k)
-        send(pool.at[slot, k], ret.at[e, k], rs.at[e], rr.at[e], sd, sp)
+        send(pool.at[slot, k], ret.at[e, k], rs.at[e], rr.at[e, k // unit], sd, sp)
 
     def experts(e, slot):
         wait(strips(e, 4), w3r.at[e])
-        wait(xr.at[e, pl.ds(1, n_src - 1)], dr.at[e])
+        wait(xr.at[e, pl.ds(0, n_src - 1)], dr.at[e])
         nt = (((1,), (1,)), ((), ()))
 
-        def send_unit(g):
-            for j in range(unit):
+        def send_unit(g, skip=0):
+            for j in range(skip, unit):
                 give_back(e, slot, g * unit + j)
 
         def work(g, rows):
@@ -160,25 +236,26 @@
             res = jnp.dot(hidden, w_v[e, 2], preferred_element_type=jnp.float32).astype(jnp.bfloat16)
             pool[slot, pl.ds(g * unit, unit)] = res.reshape(unit, cap, d_model)
 
-            @pl.when(g == 1)
-            def _():
-                for j in range(1, unit):
-                    give_back(e, slot, j)
-
-            @pl.when(g > 1)
+            @pl.when(g > 0)
             def _():
                 send_unit(g - 1)
 
         streamed(xr, e, work)
-        send_unit(units - 1)
-        pltpu.make_async_copy(pool.at[slot, 0], ret.at[e, 0], rls.at[e]).start()
+        send_unit(units - 1, 1)
+        pltpu.make_async_copy(pool.at[slot, OWN], ret.at[e, OWN], rls.at[e]).start()
 
     def wait_results_sent(e, slot):
-        wait(pool.at[slot, pl.ds(1, n_src - 1)], rs.at[e])
+        wait(pool.at[slot, pl.ds(0, n_src - 1)], rs.at[e])
 
     def combine(e):
-        wait(ret.at[e, pl.ds(1, n_src - 1)], rr.at[e])
-        pltpu.make_async_copy(pool.at[0, 0], ret.at[e, 0], rls.at[e]).wait()
+        pltpu.make_async_copy(pool.at[0, OWN], ret.at[e, OWN], rls.at[e]).wait()
+
+        def landed(g):
+            for last in range(2):
+                @pl.when((g == units - 1) if last else (g < units - 1))
+                def _(last=last):
+                    wait(ret.at[e, pl.ds(0, unit - last)], rr.at[e, g])
+
         tn = (((0,), (0,)), ((), ()))
         width = d_model // 4
 
@@ -199,17 +276,24 @@
                     total += lax.dot_general(t_v[i], cols, tn, preferred_element_type=jnp.float32)
                 acc[:, n * width:(n + 1) * width] = total
 
-        streamed(ret, e, work)
+        if isinstance(e, int):
+            arrived(ret, e, work, landed)
+        else:
+            for g in range(units):
+                landed(g)
+            streamed(ret, e, work)
 
     start_trade(0)
     start_rows(0, 0)
+    shared_stage(0)
     start_trade(1)
     start_rows(1, 1)
-    acc[...] = jnp.zeros_like(acc)
+    acc[...] = x_in[...].astype(jnp.float32)
     start_gather(0)
     start_trade(2)
     start_rows(2, 2)
     start_relay(0)
+    shared_stage(1)
     start_gather(1)
     start_trade(3)
     wait_rows_sent(0, 0)
@@ -236,16 +320,24 @@
         def _():
             start_gather(e + 2)
 
-        @pl.when(e >= 1)
+        @pl.when(e == 0)
+        def _():
+            shared_stage(2)
+
+        @pl.when(e == 1)
         def _():
             combine(e - 1)
 
         return carry
 
     lax.fori_loop(0, n_own, step, 0)
+    shared_stage(3)
+    lax.fori_loop(1, 2, lambda e, carry: combine(e) or carry, 0)
+    shared_expert()
+    lax.fori_loop(2, 3, lambda e, carry: combine(e) or carry, 0)
+    combine(n_own - 1)
     for e in range(1, n_own):
         wait_results_sent(e, (e + 1) % 3)
-    combine(n_own - 1)
 
     def drain(e, carry):
         wait(strips(e, 3), w1s.at[e])
@@ -254,9 +346,11 @@
         return carry
 
     lax.fori_loop(0, n_own, drain, 0)
-
-
-def moe(x_loc, slot, gates, wg_loc, wu_loc, wd_loc, cap):
+    for s in range(4):
+        shared_sent(s, ss)
+
+
+def moe(x_loc, slot, gates, ws_loc, wg_loc, wu_loc, wd_loc, cap):
     tok_count, d_model = x_loc.shape
     n_loc, blk, ff = wg_loc.shape
     n_exp = slot.shape[0]
@@ -268,19 +362,22 @@
     stage = jax.ShapeDtypeStruct((n_own, n_src, cap, d_model), bf16)
     return pl.pallas_call(
         moe_kernel,
-        out_shape=(jax.ShapeDtypeStruct((tok_count, d_model), jnp.float32), stage, stage),
-        in_specs=[vmem_spec] * 3 + [any_spec] * 3,
-        out_specs=(vmem_spec, any_spec, any_spec),
+        out_shape=(jax.ShapeDtypeStruct((tok_count, d_model), jnp.float32), stage, stage, jax.ShapeDtypeStruct((SIDE, 2, SIDE, SIDE) + ws_loc.shape, bf16)),
+        in_specs=[vmem_spec] * 4 + [any_spec] * 3,
+        out_specs=(vmem_spec, any_spec, any_spec, any_spec),
         scratch_shapes=[
             pltpu.VMEM((n_own, 3, ff, d_model), bf16),
             pltpu.VMEM((3, n_src, cap, d_model), bf16),
             pltpu.VMEM((2, unit, cap, d_model), bf16),
             pltpu.VMEM((3, unit * cap, tok_count), bf16),
-        ] + [dma((n_own,))] * 6 + [dma((n_own, 3))] + [dma((n_own,))] * 5 + [dma((2,)), dma((n_own,))],
+            pltpu.VMEM((2, SIDE, SIDE) + ws_loc.shape, bf16),
+            pltpu.VMEM((tok_count, ws_loc.shape[1] // 3 * 2), jnp.float32),
+            pltpu.VMEM((tok_count, ws_loc.shape[1] // 3), bf16),
+        ] + [dma((n_own,))] * 6 + [dma((n_own, 3))] + [dma((n_own,))] * 4 + [dma((n_own, n_src // unit)), dma((2,)), dma((n_own,)), dma((4,)), dma((4,)), dma, dma((2,))],
         compiler_params=pltpu.CompilerParams(has_side_effects=True, vmem_limit_bytes=65400 * 1024),
         cost_estimate=pl.CostEstimate(flops=60 * n_exp * cap * d_model * ff, bytes_accessed=100_000_000, transcendentals=n_exp * cap * ff),
         name="moe_exchange",
-    )(x_loc, slot, gates, jnp.swapaxes(wg_loc, 1, 2), jnp.swapaxes(wu_loc, 1, 2), wd_loc)[0]
+    )(x_loc, slot, gates, ws_loc, jnp.swapaxes(wg_loc, 1, 2), jnp.swapaxes(wu_loc, 1, 2), wd_loc)[0]
 
 
 def solution(mesh):
@@ -293,14 +390,10 @@
         n_exp = wg_loc.shape[0] * exp_n
         ff_shared = wsg_loc.shape[1]
         capacity = capacity_of(tok_count, idx_loc.shape[1], n_exp)
-        ws_loc = jnp.concatenate([wsg_loc, wsu_loc, wsd_loc.T], axis=1)
-        ws_all = lax.all_gather(ws_loc, group_axes, axis=0, tiled=True)
+        pad = -ff_shared % 128
+        ws_loc = jnp.concatenate([jnp.pad(w, ((0, 0), (0, pad))) for w in (wsg_loc, wsu_loc, wsd_loc.T)], axis=1)
         slot, gates = routing(idx_loc, gate_loc, n_exp, capacity)
-        routed = moe(x_loc, slot, gates, wg_loc, wu_loc, wd_loc, capacity)
-        pre = jnp.dot(x_loc, ws_all[:, :2 * ff_shared], preferred_element_type=jnp.float32)
-        s_hidden = (jax.nn.silu(pre[:, :ff_shared]) * pre[:, ff_shared:]).astype(jnp.bfloat16)
-        shared = lax.dot_general(s_hidden, ws_all[:, 2 * ff_shared:], (((1,), (1,)), ((), ())), preferred_element_type=jnp.float32)
-        return (x_loc.astype(jnp.float32) + shared + routed).astype(jnp.bfloat16)
+        return moe(x_loc, slot, gates, ws_loc, wg_loc, wu_loc, wd_loc, capacity).astype(jnp.bfloat16)
 
     in_specs = (tok_spec, tok_spec, tok_spec, P("expert", "data", None), P("expert", "data", None), P("expert", None, "data"), P(group_axes, None), P(group_axes, None), P(None, group_axes))
     return jax.shard_map(device_fn, mesh=mesh, in_specs=in_specs, out_specs=tok_spec, check_vma=False)

time: 483 us -> 464 us (0.961)
  the two profiles are of different devices: /device:TPU:1 before, /device:TPU:27 now
where the time goes in v4:
time: 464 us; the launch traced here: 463 us
  Pallas kernels  450 us (97%)
  other arithmetic  8.58 us (2%)
    pallas_call x1, Pallas kernels, moe(): pl.pallas_call(moe_kernel, out_shape=(jax.ShapeDtypeStruct((tok_count, d_...  450 us

profile of v4, /device:TPU:27, one launch (start us, length us, event | category | flops | bytes accessed | tf_op | source)
XLA Modules:
  0.0 462.7 jit_solution(14170580108670782532)
XLA Ops:
  0.0 1.4 fusion.15.ws_in
  1.4 0.8 copy.12
  2.2 2.0 fusion
  4.3 0.1 copy.13
  4.4 1.0 fusion.4.slot_in
  5.4 0.8 copy.14
  6.3 1.9 select_reduce_fusion
  8.2 0.8 copy.15
  9.0 450.4 %moe_exchange.1 = (f32[384,2048]{1,0:T(8,128)}, bf16[4,32,32,2048]{3,2,1,0:T(8,128)(2,1)}, bf16[4,32,32,2048]{3,2,1,0:T(8,128)(2,1)}, bf16[4,2,4,4,16,2304]{5,4,3,2,1,0:T(8,128)(2,1)}) custom-call(bf16[384,2048]{1,0:T(8,128)(2,1)} %x_in.1, s32[128,384]{1,0:T(8,128)} %fusion.4.slot_in, f32[128,384]{1,0:T(8,128)} %bitcast.8, bf16[16,2304]{1,0:T(8,128)(2,1)} %fusion.15.ws_in, ...), custom_call_target="tpu_custom_call" | custom-call | flops 354334801920 | bytes 100000000 | tf_op jit(solution)/shard_map/moe_exchange/pallas_call | solution.py:363
  459.4 3.3 convert_element_type.13
  (1 shorter events, 0.0 us)

commit v5 on v4

--- a/solution.py
+++ b/solution.py
@@ -324,17 +324,21 @@
         def _():
             shared_stage(2)
 
-        @pl.when(e == 1)
+        @pl.when(e == 3)
+        def _():
+            shared_expert()
+
+        @pl.when(e >= 1)
         def _():
             combine(e - 1)
 
+        @pl.when(e == 2)
+        def _():
+            shared_stage(3)
+
         return carry
 
     lax.fori_loop(0, n_own, step, 0)
-    shared_stage(3)
-    lax.fori_loop(1, 2, lambda e, carry: combine(e) or carry, 0)
-    shared_expert()
-    lax.fori_loop(2, 3, lambda e, carry: combine(e) or carry, 0)
     combine(n_own - 1)
     for e in range(1, n_own):
         wait_results_sent(e, (e + 1) % 3)

time: 464 us -> 465 us (level)
  the two profiles are of different devices: /device:TPU:27 before, /device:TPU:66 now
where the time goes in v5:
time: 465 us; the launch traced here: 464 us
  Pallas kernels  452 us (97%)
  other arithmetic  8.58 us (2%)
    pallas_call x1, Pallas kernels, moe(): pl.pallas_call(moe_kernel, out_shape=(jax.ShapeDtypeStruct((tok_count, d_...  452 us

profile of v5, /device:TPU:66, one launch (start us, length us, event | category | flops | bytes accessed | tf_op | source)
XLA Modules:
  0.0 463.8 jit_solution(9313551767008830028)
XLA Ops:
  0.0 1.4 fusion.15.ws_in
  1.4 0.8 copy.12
  2.2 2.0 fusion
  4.3 0.1 copy.13
  4.4 1.0 fusion.4.slot_in
  5.4 0.8 copy.14
  6.3 1.9 select_reduce_fusion
  8.2 0.8 copy.15
  9.0 451.5 %moe_exchange.1 = (f32[384,2048]{1,0:T(8,128)}, bf16[4,32,32,2048]{3,2,1,0:T(8,128)(2,1)}, bf16[4,32,32,2048]{3,2,1,0:T(8,128)(2,1)}, bf16[4,2,4,4,16,2304]{5,4,3,2,1,0:T(8,128)(2,1)}) custom-call(bf16[384,2048]{1,0:T(8,128)(2,1)} %x_in.1, s32[128,384]{1,0:T(8,128)} %fusion.4.slot_in, f32[128,384]{1,0:T(8,128)} %bitcast.8, bf16[16,2304]{1,0:T(8,128)(2,1)} %fusion.15.ws_in, ...), custom_call_target="tpu_custom_call" | custom-call | flops 354334801920 | bytes 100000000 | tf_op jit(solution)/shard_map/moe_exchange/pallas_call | solution.py:367
  460.5 3.3 convert_element_type.13
  (1 shorter events, 0.0 us)
